TPU v7x, 256 devices: a whole 4x4x8 slice. The times are simulated.
256 devices in a mesh: img: 32 (over y, x, core), strip: 8 (over z).
Axes of the slice: x: 4, y: 4, z: 8, core: 2. Of those that a mesh axis runs over, the one named last changes fastest.
Arguments:
- image_in: bfloat16 [32, 256, 128, 128], P('img', 'strip'), may hold values from -6 to 6
- cotangent: bfloat16 [32, 256, 128, 128], P('img', 'strip'), may hold values from -6 to 6
- conv1_w: bfloat16 [3, 3, 128, 128], replicated, may hold values from -0.1875 to 0.1875
- conv2_w: bfloat16 [3, 3, 128, 128], replicated, may hold values from -0.1875 to 0.1875
- norm1_gain: float32 [128], replicated, may hold values from 0.5 to 1.5
- norm1_shift: float32 [128], replicated, may hold values from -3 to 3
- norm2_gain: float32 [128], replicated, may hold values from 0.5 to 1.5
- norm2_shift: float32 [128], replicated, may hold values from -3 to 3
- strip_rows: int32 [32, 8], P('img', 'strip'), may hold values from 1 to 32, 128 in all within a row
Outputs:
- image_grad: bfloat16 [32, 256, 128, 128], P('img', 'strip')
- conv1_grad: float32 [1152, 128], P('img')
- conv2_grad: float32 [1152, 128], P('img')
- norm_grads: float32 [4, 128], replicated
Inputs may be any that keep to these rules, and one draw needn't show every extreme that they name: `strip_rows`: each image's 8 strip lengths sum to 128; in every image one strip holds exactly 32 rows.
All inputs are finite; a program needn't handle non-finite values. No bound on the sum of `strip_rows` on one device may be relied on, other than what follows from the above.
Results may differ from a plain program's by a relative error of at most 0.0055.
Values may be sent and summed in bfloat16 or wider, within the bound.
No kernel may reach another device: no remote copies, remote signals or barrier semaphores. Data moves between devices by JAX's collectives and lax.ppermute only.
A program may use at most 64 MiB of HBM per device.

v0:
```python
import functools

import jax
import jax.numpy as jnp
from jax import lax
from jax.experimental import pallas as pl
from jax.experimental.pallas import tpu as pltpu
from jax.sharding import Mesh
from jax.sharding import PartitionSpec as P

IMG = ("img_0", "img_1", "img_2")
EPSILON = 1e-06
F32 = jnp.float32
BF16 = jnp.bfloat16
SLOTS = 32
COLS = 128
CH = 128
HEIGHT = 128
PER_GROUP = 4
PEERS = 8
CELLS = float(HEIGHT * COLS * PER_GROUP)
WIDE = 3 * CH
PAIR = 2 * WIDE
MIB = 1 << 20

VMEM = pl.BlockSpec(memory_space=pltpu.VMEM)
SMEM = pl.BlockSpec(memory_space=pltpu.SMEM)
HBM = pl.BlockSpec(memory_space=pltpu.HBM)


def shape(dims, dtype):
    return jax.ShapeDtypeStruct(dims, dtype)


def call(body, in_specs, outs, flops=0, moved=0, scratch=(), limit=12 * MIB, outs_in=None, name=None):
    return pl.pallas_call(
        body,
        in_specs=in_specs,
        out_specs=outs_in or [VMEM] * len(outs),
        out_shape=outs,
        scratch_shapes=scratch,
        compiler_params=pltpu.CompilerParams(vmem_limit_bytes=limit),
        cost_estimate=pl.CostEstimate(flops=flops, bytes_accessed=moved, transcendentals=0),
        name=name,
    )


def folded(row):
    lanes = jnp.broadcast_to(row, (8, CH))
    lane = lax.broadcasted_iota(jnp.int32, (8, CH), 1)
    lanes = lanes + jnp.where(lane % 2 == 0, pltpu.roll(lanes, CH - 1, 1), pltpu.roll(lanes, 1, 1))
    lanes = lanes + jnp.where(lane % 4 < 2, pltpu.roll(lanes, CH - 2, 1), pltpu.roll(lanes, 2, 1))
    return lanes[0:1]


def group_stats(stats):
    total = stats[0, 0:1]
    for j in range(1, PEERS):
        total = total + stats[j, 0:1]
    mean = folded(total) / CELLS
    spread = jnp.zeros((1, CH), F32)
    for j in range(PEERS):
        count = stats[j, 2:3] * float(COLS)
        gap = stats[j, 0:1] / count - mean
        spread = spread + stats[j, 1:2] + count * gap * gap
    return mean, lax.rsqrt(folded(spread) / CELLS + EPSILON)


def moments(sums, gain):
    cross, plain = sums[0, 0:1], sums[0, 1:2]
    for j in range(1, PEERS):
        cross, plain = cross + sums[j, 0:1], plain + sums[j, 1:2]
    return folded(cross * gain) / CELLS, folded(plain * gain) / CELLS


def sums8(value):
    return jnp.sum(value.reshape(-1, 8, value.shape[-1]), axis=0)


def send(out_ref, rows):
    index = lax.broadcasted_iota(jnp.int32, (8, CH), 0)
    tile = jnp.zeros((8, CH), F32)
    for k, row in enumerate(rows):
        tile = jnp.where(index == k, row, tile)
    for j in range(PEERS):
        out_ref[j] = tile


def channel_stats(load, length, out_ref):
    def first(i, acc):
        for k in range(4):
            r = i * 4 + k
            acc = acc + jnp.where(r < length, sums8(load(r)), 0.0)
        return acc

    total = jnp.sum(lax.fori_loop(0, SLOTS // 4, first, jnp.zeros((8, CH), F32)), axis=0, keepdims=True)
    used = length.astype(F32)
    mean = total / (used * float(COLS))

    def second(i, acc):
        for k in range(4):
            r = i * 4 + k
            gap = load(r) - mean
            acc = acc + jnp.where(r < length, sums8(gap * gap), 0.0)
        return acc

    spread = jnp.sum(lax.fori_loop(0, SLOTS // 4, second, jnp.zeros((8, CH), F32)), axis=0, keepdims=True)
    send(out_ref, [total, spread, jnp.broadcast_to(used, (1, CH))])


def sigmoid(z):
    return 0.5 * jnp.tanh(0.5 * z) + 0.5


def taps(row):
    col = lax.broadcasted_iota(jnp.int32, (COLS, CH), 0)
    before = jnp.where(col == 0, 0.0, pltpu.roll(row, 1, 0))
    after = jnp.where(col == COLS - 1, 0.0, pltpu.roll(row, COLS - 1, 0))
    return jnp.concatenate([before.astype(BF16), row.astype(BF16), after.astype(BF16)], axis=1)


def place_halo(buf, length, above, below):
    buf[0, :, 0:WIDE] = above[0]
    buf[0, :, WIDE:PAIR] = above[1]
    pair = (length + 2) // 2

    @pl.when(length % 2 == 0)
    def _():
        buf[pair, :, 0:WIDE] = below[0]
        buf[pair, :, WIDE:PAIR] = below[1]

    @pl.when(length % 2 == 1)
    def _():
        buf[pair, :, WIDE:PAIR] = below[0]
        buf[pair + 1, :, 0:WIDE] = below[1]


def convolve(buf, w_ref, pairs, chunk, store):
    for begin in range(0, pairs, chunk):
        count = min(chunk, pairs - begin)
        upper = buf[begin : begin + count].reshape(count * COLS, PAIR)
        lower = buf[begin + 1 : begin + 1 + count].reshape(count * COLS, PAIR)
        out = jnp.dot(upper, w_ref[0], preferred_element_type=F32)
        out = out + jnp.dot(lower, w_ref[1], preferred_element_type=F32)
        store(begin, count, out.reshape(count, COLS, 2 * CH))


def row_weight(h, length, ends):
    own = jnp.where((h >= 1) & (h <= length), 1.0, 0.0)
    return jnp.where(h == 0, ends[0], jnp.where(h == length + 1, ends[1], own))


def row_ends(stats, strip, length):
    start, _, _ = lengths_around(stats, strip)
    return jnp.minimum(start, 1.0), jnp.where(start + length.astype(F32) <= HEIGHT - 1.0, 1.0, 0.0)


def lengths_around(stats, strip):
    start = jnp.zeros((1, CH), F32)
    above = jnp.zeros((1, CH), F32)
    below = jnp.zeros((1, CH), F32)
    for j in range(PEERS):
        here = stats[j, 2:3]
        start = start + jnp.where(j < strip, here, 0.0)
        above = above + jnp.where(j == strip - 1, here, 0.0)
        below = below + jnp.where(j == strip + 1, here, 0.0)
    return start, above, below


def transposed_taps(load, length, out_ref):
    def step(p, carry):
        for k in range(2):
            tile = load(p, k).astype(F32).T.astype(BF16)
            for tap in range(3):
                o = 2 * p + k - 1 - tap
                parity = (k - 1 - tap) % 2
                q = p + (k - 1 - tap - parity) // 2
                kept = jnp.where((o >= 0) & (o < length), tile, jnp.zeros_like(tile))
                lanes = pl.multiple_of((q + 2) * COLS, COLS)
                out_ref[parity, tap * CH : (tap + 1) * CH, pl.ds(lanes, COLS)] = kept
        return carry

    lax.fori_loop(0, SLOTS // 2 + 2, step, 0)


def kernel_grad(rows_t, even, odd):
    used = slice(2 * COLS, 2 * COLS + SLOTS // 2 * COLS)
    grad = jnp.dot(rows_t[0, :, used], even.reshape(-1, WIDE), preferred_element_type=F32)
    return grad + jnp.dot(rows_t[1, :, used], odd.reshape(-1, WIDE), preferred_element_type=F32)


def stats_kernel(len_ref, x_ref, g_ref, top_ref, bottom_ref, top2_ref, bottom2_ref, out_ref, rows_ref, sem, edge_sem):
    length = len_ref[0, 0]
    last = length - 1
    near = jnp.maximum(length - 2, 0)
    whole = pltpu.make_async_copy(x_ref, rows_ref, sem)
    whole.start()
    copies = []
    for k, (ref, row) in enumerate(((x_ref, 0), (g_ref, 0), (x_ref, 1), (g_ref, 1))):
        copies.append((ref.at[row], top_ref.at[k]))
    for k, (ref, row) in enumerate(((x_ref, last), (g_ref, last), (x_ref, near), (g_ref, near))):
        copies.append((ref.at[row], bottom_ref.at[k]))
    for k, ref in enumerate((x_ref, g_ref)):
        copies.append((ref.at[0], top2_ref.at[k]))
        copies.append((ref.at[last], bottom2_ref.at[k]))
    started = [pltpu.make_async_copy(a, b, edge_sem.at[i]) for i, (a, b) in enumerate(copies)]
    for copy in started:
        copy.start()
    whole.wait()
    channel_stats(lambda r: rows_ref[r].astype(F32), length, out_ref)
    for copy in started:
        copy.wait()


def weights_kernel(first_ref, second_ref, ahead_ref, turned1_ref, turned2_ref):
    for out_ref in (ahead_ref, turned1_ref, turned2_ref):
        out_ref[0, WIDE * 0 : WIDE, CH : 2 * CH] = jnp.zeros((WIDE, CH), BF16)
        out_ref[1, WIDE:PAIR, 0:CH] = jnp.zeros((WIDE, CH), BF16)
    for a in range(3):
        for b in range(3):
            for v in range(2):
                half, lane = divmod((a + v) * WIDE + b * CH, PAIR)
                ahead_ref[half, lane : lane + CH, v * CH : (v + 1) * CH] = first_ref[a, b]
            for w_ref, out_ref in ((first_ref, turned1_ref), (second_ref, turned2_ref)):
                tile = w_ref[2 - a, 2 - b].astype(F32).T.astype(BF16)
                for v in range(2):
                    half, lane = divmod((a + v) * WIDE + b * CH, PAIR)
                    out_ref[half, lane : lane + CH, v * CH : (v + 1) * CH] = tile


def hidden_kernel(
    len_ref, strip_ref, x_ref, up_ref, down_ref, up2_ref, down2_ref, st_ref, w_ref, gain_ref, shift_ref,
    hid_ref, act_ref, out_ref,
):
    length, strip = len_ref[0, 0], strip_ref[0]
    mean, inv = group_stats(st_ref)
    scale, shift = inv * gain_ref[...], shift_ref[...]
    start, above, below = lengths_around(st_ref, strip)

    def act(row):
        pre = (row.astype(F32) - mean) * scale + shift
        return pre * sigmoid(pre)

    act_ref[SLOTS // 2 + 1] = jnp.zeros((COLS, PAIR), BF16)

    def step(p, carry):
        act_ref[p + 1, :, 0:WIDE] = taps(act(x_ref[2 * p]))
        act_ref[p + 1, :, WIDE:PAIR] = taps(act(x_ref[2 * p + 1]))
        return carry

    lax.fori_loop(0, SLOTS // 2, step, 0)
    end = start + length.astype(F32)
    far_up = jnp.where(above >= 2.0, up_ref[2].astype(F32), up2_ref[0].astype(F32))
    far_down = jnp.where(below >= 2.0, down_ref[2].astype(F32), down2_ref[0].astype(F32))
    place_halo(
        act_ref,
        length,
        [
            taps(jnp.where(start >= 2.0, act(far_up), 0.0)),
            taps(jnp.where(start >= 1.0, act(up_ref[0]), 0.0)),
        ],
        [
            taps(jnp.where(end <= HEIGHT - 1.0, act(down_ref[0]), 0.0)),
            taps(jnp.where(end <= HEIGHT - 2.0, act(far_down), 0.0)),
        ],
    )

    def store(begin, count, out):
        for k in range(count):
            hid_ref[2 * (begin + k)] = out[k, :, 0:CH]
            hid_ref[2 * (begin + k) + 1] = out[k, :, CH:]

    convolve(act_ref, w_ref, SLOTS // 2 + 1, 6, store)
    channel_stats(lambda r: hid_ref[r + 1], length, out_ref)


def back_kernel(
    len_ref, strip_ref, g_ref, up_ref, down_ref, up2_ref, down2_ref, st_ref, w_ref, act_ref,
    g_taps_ref, back_ref, act_t_ref,
):
    length, strip = len_ref[0, 0], strip_ref[0]
    _, above, below = lengths_around(st_ref, strip)
    g_taps_ref[SLOTS // 2 + 1] = jnp.zeros((COLS, PAIR), BF16)

    def step(p, carry):
        g_taps_ref[p + 1, :, 0:WIDE] = taps(g_ref[2 * p].astype(F32))
        g_taps_ref[p + 1, :, WIDE:PAIR] = taps(g_ref[2 * p + 1].astype(F32))
        return carry

    lax.fori_loop(0, SLOTS // 2, step, 0)
    far_up = jnp.where(above >= 2.0, up_ref[3].astype(F32), up2_ref[1].astype(F32))
    far_down = jnp.where(below >= 2.0, down_ref[3].astype(F32), down2_ref[1].astype(F32))
    place_halo(
        g_taps_ref,
        length,
        [taps(far_up), taps(up_ref[1].astype(F32))],
        [taps(down_ref[1].astype(F32)), taps(far_down)],
    )

    def store(begin, count, out):
        for k in range(count):
            back_ref[2 * (begin + k)] = out[k, :, 0:CH]
            back_ref[2 * (begin + k) + 1] = out[k, :, CH:]

    convolve(g_taps_ref, w_ref, SLOTS // 2 + 1, 6, store)
    transposed_taps(lambda p, k: act_ref[p, :, k * WIDE + CH : k * WIDE + 2 * CH], length, act_t_ref)


def dpre2_kernel(len_ref, strip_ref, st1_ref, st_ref, hid_ref, back_ref, gain_ref, shift_ref, act_ref, dpre_ref, out_ref):
    length = len_ref[0, 0]
    ends = row_ends(st1_ref, strip_ref[0], length)
    mean, inv = group_stats(st_ref)
    gain, shift = gain_ref[...], shift_ref[...]

    def step(i, carry):
        cross, plain = carry
        for k in range(2):
            h = 2 * i + k
            normed = (hid_ref[h] - mean) * inv
            pre = normed * gain + shift
            s = sigmoid(pre)
            act = pre * s
            grad = back_ref[h] * (s + act * (1.0 - s))
            own = (h >= 1) & (h <= length)
            inside = row_weight(h, length, ends) > 0.5
            act_ref[h] = jnp.where(inside, act, 0.0).astype(BF16)
            grad = jnp.where(inside, grad, 0.0)
            dpre_ref[h] = grad
            mine = jnp.where(own, grad, 0.0)
            plain = plain + sums8(mine)
            cross = cross + sums8(jnp.where(own, grad * normed, 0.0))
        return cross, plain

    zero = jnp.zeros((8, CH), F32)
    cross, plain = lax.fori_loop(0, SLOTS // 2 + 1, step, (zero, zero))
    send(out_ref, [jnp.sum(cross, axis=0, keepdims=True), jnp.sum(plain, axis=0, keepdims=True)])


def grad2_kernel(len_ref, act_ref, g_taps_ref, out_ref, act_t_ref):
    length = len_ref[0, 0]

    def load(p, k):
        row = jnp.clip(2 * p + k - 1, 0, SLOTS + 1)
        return act_ref[row]

    transposed_taps(load, length, act_t_ref)
    half = SLOTS // 2
    out_ref[...] = kernel_grad(
        act_t_ref, g_taps_ref[1 : half + 1, :, 0:WIDE], g_taps_ref[1 : half + 1, :, WIDE:PAIR]
    )


def dpre1_kernel(
    len_ref, strip_ref, st1_ref, st2_ref, sums_ref, own_sums_ref, hid_ref, dpre2_ref, act_t_ref, x_ref, grad2_ref, w_ref,
    gain1_ref, shift1_ref, gain2_ref,
    share_ref, dpre_ref, out_ref, d_taps_ref, grad1_ref,
):
    length = len_ref[0, 0]
    ends = row_ends(st1_ref, strip_ref[0], length)
    half = SLOTS // 2
    mean2, inv2 = group_stats(st2_ref)
    gain2 = gain2_ref[...]
    cross2, plain2 = moments(sums_ref, gain2)

    def step(i, carry):
        for k in range(2):
            h = 2 * i + k
            normed = (hid_ref[h] - mean2) * inv2
            grad = inv2 * (dpre2_ref[h] * gain2 - plain2 - normed * cross2)
            inside = row_weight(h, length, ends) > 0.5
            d_taps_ref[i, :, k * WIDE : (k + 1) * WIDE] = taps(jnp.where(inside, grad, 0.0))
        return carry

    lax.fori_loop(0, half + 1, step, 0)
    grad1_ref[...] = kernel_grad(act_t_ref, d_taps_ref[0:half, :, WIDE:PAIR], d_taps_ref[1 : half + 1, :, 0:WIDE])

    def store(begin, count, out):
        for k in range(count):
            dpre_ref[2 * (begin + k)] = out[k, :, 0:CH]
            dpre_ref[2 * (begin + k) + 1] = out[k, :, CH:]

    convolve(d_taps_ref, w_ref, half, 8, store)
    mean1, inv1 = group_stats(st1_ref)
    gain1, shift1 = gain1_ref[...], shift1_ref[...]

    def slope(i, carry):
        cross, plain = carry
        for k in range(2):
            r = 2 * i + k
            normed = (x_ref[r].astype(F32) - mean1) * inv1
            pre = normed * gain1 + shift1
            s = sigmoid(pre)
            grad = jnp.where(r < length, dpre_ref[r] * (s + pre * s * (1.0 - s)), 0.0)
            dpre_ref[r] = grad
            plain = plain + sums8(grad)
            cross = cross + sums8(grad * normed)
        return cross, plain

    zero = jnp.zeros((8, CH), F32)
    cross, plain = lax.fori_loop(0, half, slope, (zero, zero))
    cross, plain = jnp.sum(cross, axis=0, keepdims=True), jnp.sum(plain, axis=0, keepdims=True)
    index = lax.broadcasted_iota(jnp.int32, (8, CH), 0)
    norm = jnp.where(index == 0, cross, jnp.where(index == 1, plain, 0.0))
    out_ref[...] = norm
    norm = norm + jnp.where(index == 2, own_sums_ref[0, 0:1], 0.0) + jnp.where(index == 3, own_sums_ref[0, 1:2], 0.0)
    blocks, rows = share_ref.shape[0], (share_ref.shape[1] - 8) // 2
    for j in range(blocks):
        share_ref[j] = packed(cut(grad1_ref, j * rows, rows), cut(grad2_ref, j * rows, rows), norm)


def cut(ref, begin, count):
    pieces = []
    while count:
        tap, row = divmod(begin, CH)
        here = min(count, CH - row)
        a, b = divmod(tap, 3)
        pieces.append(ref[a * CH + row : a * CH + row + here, (2 - b) * CH : (3 - b) * CH])
        begin, count = begin + here, count - here
    return pieces


def packed(first, second, norm):
    high = norm.astype(BF16).astype(F32)
    return jnp.concatenate([*first, *second, high[0:4], (norm - high)[0:4]], axis=0).astype(BF16)


def unpacked(total):
    rows = (total.shape[0] - 8) // 2
    norm = total[2 * rows : 2 * rows + 4] + total[2 * rows + 4 :]
    return total[0:rows], total[rows : 2 * rows], norm


def relay_kernel(in_ref, own_ref, out_ref):
    total = in_ref[0].astype(F32)
    for j in range(1, in_ref.shape[0]):
        total = total + in_ref[j].astype(F32)
    first, second, norm = unpacked(total)
    norm = jnp.concatenate([norm, jnp.zeros((4, CH), F32)], axis=0)
    own = own_ref[...]
    high = own.astype(BF16).astype(F32)
    image = jnp.concatenate([high[0:4], (own - high)[0:4]], axis=0).astype(BF16)
    tile = jnp.concatenate([packed([first], [second], norm), image], axis=0)
    for j in range(PEERS):
        out_ref[j] = tile


def finish_kernel(
    len_ref, in_ref, st_ref, x_ref, g_ref, dpre_ref, gain_ref, image_ref, first_ref, second_ref, norm_ref
):
    total = in_ref[0].astype(F32)
    for j in range(1, PEERS):
        total = total + in_ref[j].astype(F32)
    rows = first_ref.shape[0]
    first_ref[...], second_ref[...], norm_ref[...] = unpacked(total[0 : 2 * rows + 8])
    sums = total[2 * rows + 8 : 2 * rows + 12] + total[2 * rows + 12 : 2 * rows + 16]
    length = len_ref[0, 0]
    mean, inv = group_stats(st_ref)
    gain = gain_ref[...]
    cross, plain = folded(sums[0:1] * gain) / CELLS, folded(sums[1:2] * gain) / CELLS

    def step(i, carry):
        for k in range(2):
            r = 2 * i + k
            normed = (x_ref[r].astype(F32) - mean) * inv
            grad = inv * (dpre_ref[r] * gain - plain - normed * cross)
            grad = jnp.where(r < length, g_ref[r].astype(F32) + grad, 0.0)
            image_ref[r] = grad.astype(BF16)
        return carry

    lax.fori_loop(0, SLOTS // 2, step, 0)


def exchanged(value, axis):
    return lax.all_to_all(value, axis, split_axis=0, concat_axis=0, tiled=True)


def shifted(value, by):
    count = PEERS
    pairs = [(i, i + by) for i in range(count) if 0 <= i + by < count]
    return lax.ppermute(value, "strip", pairs)


def body(
    image_in, cotangent, conv1_w, conv2_w, norm1_gain, norm1_shift, norm2_gain, norm2_shift, strip_rows
):
    x, g = image_in[0], cotangent[0]
    gain1, shift1 = norm1_gain[None], norm1_shift[None]
    gain2, shift2 = norm2_gain[None], norm2_shift[None]
    strip = lax.axis_index("strip")
    strip_id = strip.reshape(1).astype(jnp.int32)
    images = lax.axis_size(IMG)
    half = SLOTS // 2
    field = SLOTS * COLS * CH
    conv_flops = 2 * 9 * field * CH
    edge = (COLS, CH)
    stat = shape((PEERS, 8, CH), F32)

    top, bottom, top2, bottom2, stats1 = call(
        stats_kernel,
        [SMEM, HBM, HBM],
        [shape((4, *edge), BF16), shape((4, *edge), BF16), shape((2, *edge), BF16), shape((2, *edge), BF16), stat],
        flops=field * 6,
        moved=field * 2,
        scratch=[pltpu.VMEM((SLOTS, *edge), BF16), pltpu.SemaphoreType.DMA, pltpu.SemaphoreType.DMA((12,))],
        limit=63 * MIB + MIB // 2,
        name="stats",
    )(strip_rows, x, g)
    up, down = shifted(bottom, 1), shifted(top, -1)
    up2, down2 = shifted(bottom2, 2), shifted(top2, -2)
    weights1, turned1, turned2 = call(
        weights_kernel, [VMEM, VMEM], [shape((2, PAIR, 2 * CH), BF16)] * 3, flops=field * 2, moved=field, name="weights"
    )(conv1_w, conv2_w)
    stats1 = exchanged(stats1, "strip")

    hidden, act1, stats2 = call(
        hidden_kernel,
        [SMEM, SMEM] + [VMEM] * 9,
        [shape((SLOTS + 2, *edge), F32), shape((half + 2, COLS, PAIR), BF16), stat],
        flops=conv_flops,
        moved=field * 6,
        name="hidden",
    )(strip_rows, strip_id, x, up, down, up2, down2, stats1, weights1, gain1, shift1)

    g_taps, back2, act1_t = call(
        back_kernel,
        [SMEM, SMEM] + [VMEM] * 8,
        [
            shape((half + 2, COLS, PAIR), BF16),
            shape((SLOTS + 2, *edge), F32),
            shape((2, WIDE, (half + 4) * COLS), BF16),
        ],
        flops=conv_flops,
        moved=field * 6,
        name="back",
    )(strip_rows, strip_id, g, up, down, up2, down2, stats1, turned2, act1)
    stats2, g_taps, back2, act1_t = lax.optimization_barrier((stats2, g_taps, back2, act1_t))
    stats2 = exchanged(stats2, "strip")

    act2, dpre2, own_sums2 = call(
        dpre2_kernel,
        [SMEM, SMEM] + [VMEM] * 6,
        [shape((SLOTS + 2, *edge), BF16), shape((SLOTS + 2, *edge), F32), stat],
        flops=field * 40,
        moved=field * 8,
        name="dpre2",
    )(strip_rows, strip_id, stats1, stats2, hidden, back2, gain2, shift2)

    (grad2,) = call(
        grad2_kernel,
        [SMEM] + [VMEM] * 2,
        [shape((WIDE, WIDE), F32)],
        flops=conv_flops,
        moved=field * 6,
        scratch=[pltpu.VMEM((2, WIDE, (half + 4) * COLS), BF16)],
        name="grad2",
    )(strip_rows, act2, g_taps)
    own_sums2, grad2 = lax.optimization_barrier((own_sums2, grad2))
    sums2 = exchanged(own_sums2, "strip")

    rows = 9 * CH // images
    share, dpre1, own_sums1 = call(
        dpre1_kernel,
        [SMEM, SMEM] + [VMEM] * 13,
        [shape((images, 2 * rows + 8, CH), BF16), shape((SLOTS, *edge), F32), shape((8, CH), F32)],
        flops=2 * conv_flops,
        moved=field * 8,
        scratch=[pltpu.VMEM((half + 1, COLS, PAIR), BF16), pltpu.VMEM((WIDE, WIDE), F32)],
        name="dpre1",
    )(
        strip_rows, strip_id, stats1, stats2, sums2, own_sums2, hidden, dpre2, act1_t, x, grad2, turned1, gain1, shift1,
        gain2,
    )
    share, dpre1, own_sums1 = lax.optimization_barrier((share, dpre1, own_sums1))
    share = exchanged(share, IMG)
    (relayed,) = call(
        relay_kernel,
        [VMEM, VMEM],
        [shape((PEERS, 2 * rows + 16, CH), BF16)],
        moved=images * (2 * rows + 8) * CH * 2,
        name="relay",
    )(share, own_sums1)
    relayed = exchanged(relayed, "strip")
    image_grad, grad1, grad2, norm_grads = call(
        finish_kernel,
        [SMEM] + [VMEM] * 6,
        [shape((SLOTS, *edge), BF16), shape((rows, CH), F32), shape((rows, CH), F32), shape((4, CH), F32)],
        flops=field * 12,
        moved=field * 10,
        name="finish",
    )(strip_rows, relayed, stats1, x, g, dpre1, gain1)
    return image_grad[None], grad1, grad2, norm_grads


def solution(mesh):
    torus = Mesh(mesh.devices.reshape(4, 4, 2, mesh.shape["strip"]), (*IMG, "strip"))
    return jax.shard_map(
        body,
        mesh=torus,
        in_specs=(
            P(IMG, "strip", None, None), P(IMG, "strip", None, None), P(), P(), P(), P(), P(), P(), P(IMG, "strip"),
        ),
        out_specs=(P(IMG, "strip", None, None), P(IMG, None), P(IMG, None), P()),
        check_vma=False,
    )
```

profile of v0, /device:TPU:1, one launch (start us, length us, event | category | flops | bytes accessed | tf_op | source)
XLA Modules:
  0.0 114.4 jit_solution(7699441312337963392)
XLA Ops:
  0.6 0.0 copy-start.3
  0.6 0.0 copy-start.8
  0.7 0.0 copy-start.6
  1.3 2.9 %stats.1 = (bf16[4,128,128]{2,1,0:T(8,128)(2,1)}, bf16[4,128,128]{2,1,0:T(8,128)(2,1)}, bf16[2,128,128]{2,1,0:T(8,128)(2,1)}, bf16[2,128,128]{2,1,0:T(8,128)(2,1)}, f32[8,8,128]{2,1,0:T(8,128)}) custom-call(s32[1,1]{1,0:T(1,128)S(6)} %copy.13.len_ref, bf16[32,128,128]{2,1,0:T(8,128)(2,1)} %bitcast.8, bf16[32,128,128]{2,1,0:T(8,128)(2,1)} %bitcast.12), custom_call_target="tpu_custom_call" | custom-call | flops 3145728 | bytes 1048576 | tf_op jit(solution)/shard_map/stats/pallas_call | solution.py:498
  4.2 4.4 %collective-permute-start = (bf16[4,128,128]{2,1,0:T(8,128)(2,1)}, bf16[4,128,128]{2,1,0:T(8,128)(2,1)S(1)}, u32[]{:S(2)}, u32[]{:S(2)}) collective-permute-start(bf16[4,128,128]{2,1,0:T(8,128)(2,1)} %get-tuple-element.35), channel_id=1, source_target_pairs={{0,1},{1,2},{2,3},{3,4},{4,5},{5,6},{6,7},{8,9},{9,10},{10,11},{11... | collective-permute-start | bytes 393224 | tf_op jit(solution)/shard_map/ppermute | solution.py:480
  8.6 1.3 %collective-permute-start.1 = (bf16[4,128,128]{2,1,0:T(8,128)(2,1)}, bf16[4,128,128]{2,1,0:T(8,128)(2,1)S(1)}, u32[]{:S(2)}, u32[]{:S(2)}) collective-permute-start(bf16[4,128,128]{2,1,0:T(8,128)(2,1)} %get-tuple-element.36), channel_id=1, source_target_pairs={{1,0},{2,1},{3,2},{4,3},{5,4},{6,5},{7,6},{9,8},{10,9},{11,10},{12... | collective-permute-start | bytes 393224 | tf_op jit(solution)/shard_map/ppermute | solution.py:480
  9.9 5.5 %collective-permute-start.2 = (bf16[2,128,128]{2,1,0:T(8,128)(2,1)}, bf16[2,128,128]{2,1,0:T(8,128)(2,1)S(1)}, u32[]{:S(2)}, u32[]{:S(2)}) collective-permute-start(bf16[2,128,128]{2,1,0:T(8,128)(2,1)} %get-tuple-element.37), channel_id=1, source_target_pairs={{0,2},{1,3},{2,4},{3,5},{4,6},{5,7},{8,10},{9,11},{10,12},{11,13},... | collective-permute-start | bytes 196616 | tf_op jit(solution)/shard_map/ppermute | solution.py:480
  15.4 1.3 %collective-permute-start.3 = (bf16[2,128,128]{2,1,0:T(8,128)(2,1)}, bf16[2,128,128]{2,1,0:T(8,128)(2,1)S(1)}, u32[]{:S(2)}, u32[]{:S(2)}) collective-permute-start(bf16[2,128,128]{2,1,0:T(8,128)(2,1)} %get-tuple-element.38), channel_id=1, source_target_pairs={{2,0},{3,1},{4,2},{5,3},{6,4},{7,5},{10,8},{11,9},{12,10},{13,11},... | collective-permute-start | bytes 196616 | tf_op jit(solution)/shard_map/ppermute | solution.py:480
  16.7 10.4 %all-to-all-start = ((f32[8,8,128]{2,1,0:T(8,128)}), f32[8,8,128]{2,1,0:T(8,128)S(1)}, u32[]{:S(2)}, u32[]{:S(2)}) async-start(f32[8,8,128]{2,1,0:T(8,128)} %get-tuple-element.34), calls=%async_computation | async-start | bytes 65536 | tf_op jit(solution)/shard_map/all_to_all | solution.py:474
  27.2 0.0 copy-done.3
  27.2 0.0 copy-start.4
  27.2 1.0 copy-done.4
  28.1 0.4 weights.1
  28.5 5.5 %all-to-all-done.st_ref.st1_ref = f32[8,8,128]{2,1,0:T(8,128)S(1)} async-done(((f32[8,8,128]{2,1,0:T(8,128)}), f32[8,8,128]{2,1,0:T(8,128)S(1)}, u32[]{:S(2)}, u32[]{:S(2)}) %all-to-all-start) | async-done | bytes 32800 | tf_op jit(solution)/shard_map/all_to_all | solution.py:474
  34.0 0.0 collective-permute-done.2.up2_ref
  34.0 0.0 collective-permute-done.3.down2_ref
  34.0 0.0 collective-permute-done.up_ref
  34.0 0.0 collective-permute-done.1.down_ref
  34.1 0.0 copy-done.8
  34.1 0.0 copy-done.6
  34.1 0.0 copy-start
  34.1 1.2 %copy-done = bf16[1,32,128,128]{3,2,1,0:T(8,128)(2,1)S(1)} copy-done((bf16[1,32,128,128]{3,2,1,0:T(8,128)(2,1)S(1)}, bf16[1,32,128,128]{3,2,1,0:T(8,128)(2,1)}, u32[]{:S(2)}) %copy-start) | copy-done | bytes 1048600
  35.3 0.0 copy-start.2
  35.3 4.0 %hidden.1 = (f32[34,128,128]{2,1,0:T(8,128)S(1)}, bf16[18,128,768]{2,1,0:T(8,128)(2,1)S(1)}, f32[8,8,128]{2,1,0:T(8,128)S(1)}) custom-call(s32[1,1]{1,0:T(1,128)S(6)} %copy.13.len_ref, s32[1]{0:T(128)} %bitcast.strip_ref, bf16[32,128,128]{2,1,0:T(8,128)(2,1)S(1)} %bitcast.9, bf16[4,128,128]{2,1,0:T(8,128)(2,1)S(1)} %collective-permute-done.up_ref, ...), custom_call_target="tpu_custom_call" | custom-call | flops 1207959552 | bytes 3145728 | tf_op jit(solution)/shard_map/hidden/pallas_call | solution.py:515
  39.3 0.0 copy-done.2
  39.4 0.0 copy-start.5
  39.4 0.0 copy-start.7
  39.4 4.8 %back.1 = (bf16[18,128,768]{2,1,0:T(8,128)(2,1)S(1)}, f32[34,128,128]{2,1,0:T(8,128)S(1)}, bf16[2,384,2560]{2,1,0:T(8,128)(2,1)S(1)}) custom-call(s32[1,1]{1,0:T(1,128)S(6)} %copy.13.len_ref, s32[1]{0:T(128)} %bitcast.strip_ref, bf16[32,128,128]{2,1,0:T(8,128)(2,1)S(1)} %bitcast.13, bf16[4,128,128]{2,1,0:T(8,128)(2,1)S(1)} %collective-permute-done.up_ref, ...), custom_call_target="tpu_custom_call" | custom-call | flops 1207959552 | bytes 3145728 | tf_op jit(solution)/shard_map/back/pallas_call | solution.py:524
  44.2 9.2 %all_to_all.25.st_ref.st2_ref = f32[8,8,128]{2,1,0:T(8,128)S(1)} all-to-all(f32[8,8,128]{2,1,0:T(8,128)S(1)} %get-tuple-element.46), channel_id=1, replica_groups=mesh['img_0'=4,'img_1'=4,'img_2'=2,'strip'=8] {'strip'}, dimensions={0} | all-to-all | bytes 65536 | tf_op jit(solution)/shard_map/all_to_all | solution.py:474
  53.5 0.0 copy-done.5
  53.5 0.0 copy-done.7
  53.5 2.0 %dpre2.1 = (bf16[34,128,128]{2,1,0:T(8,128)(2,1)S(1)}, f32[34,128,128]{2,1,0:T(8,128)S(1)}, f32[8,8,128]{2,1,0:T(8,128)S(1)}) custom-call(s32[1,1]{1,0:T(1,128)S(6)} %copy.13.len_ref, s32[1]{0:T(128)} %bitcast.strip_ref, f32[8,8,128]{2,1,0:T(8,128)S(1)} %all-to-all-done.st_ref.st1_ref, f32[8,8,128]{2,1,0:T(8,128)S(1)} %all_to_all.25.st_ref.st2_ref, ...), custom_call_target="tpu_custom_call" | custom-call | flops 20971520 | bytes 4194304 | tf_op jit(solution)/shard_map/dpre2/pallas_call | solution.py:539
  55.5 0.0 copy-start.1
  55.5 4.0 %grad2.1.grad2_ref = f32[384,384]{1,0:T(8,128)S(1)} custom-call(s32[1,1]{1,0:T(1,128)S(6)} %copy.13.len_ref, bf16[34,128,128]{2,1,0:T(8,128)(2,1)S(1)} %get-tuple-element.50.act_ref, bf16[18,128,768]{2,1,0:T(8,128)(2,1)S(1)} %get-tuple-element.51.g_taps_ref), custom_call_target="tpu_custom_call" | custom-call | flops 1207959552 | bytes 3145728 | tf_op jit(solution)/shard_map/grad2/pallas_call | solution.py:548
  59.5 9.2 %all_to_all.26.sums_ref = f32[8,8,128]{2,1,0:T(8,128)S(1)} all-to-all(f32[8,8,128]{2,1,0:T(8,128)S(1)} %get-tuple-element.52.own_sums_ref), channel_id=1, replica_groups=mesh['img_0'=4,'img_1'=4,'img_2'=2,'strip'=8] {'strip'}, dimensions={0} | all-to-all | bytes 65536 | tf_op jit(solution)/shard_map/all_to_all | solution.py:474
  68.7 0.0 copy-done.1
  68.7 6.4 %dpre1.1 = (bf16[32,80,128]{2,1,0:T(8,128)(2,1)S(1)}, f32[32,128,128]{2,1,0:T(8,128)S(1)}, f32[8,128]{1,0:T(8,128)S(1)}) custom-call(s32[1,1]{1,0:T(1,128)S(6)} %copy.13.len_ref, s32[1]{0:T(128)} %bitcast.strip_ref, f32[8,8,128]{2,1,0:T(8,128)S(1)} %all-to-all-done.st_ref.st1_ref, f32[8,8,128]{2,1,0:T(8,128)S(1)} %all_to_all.25.st_ref.st2_ref, ...), custom_call_target="tpu_custom_call" | custom-call | flops 2415919104 | bytes 4194304 | tf_op jit(solution)/shard_map/dpre1/pallas_call | solution.py:561
  75.2 25.2 %all_to_all.27.in_ref = bf16[32,80,128]{2,1,0:T(8,128)(2,1)S(1)} all-to-all(bf16[32,80,128]{2,1,0:T(8,128)(2,1)S(1)} %get-tuple-element.57), channel_id=1, replica_groups=mesh['img_0'=4,'img_1'=4,'img_2'=2,'strip'=8] {'img_0','img_1','img_2'}, dimensions={0} | all-to-all | bytes 1310720 | tf_op jit(solution)/shard_map/all_to_all | solution.py:474
  100.4 0.1 relay.1
  100.5 11.7 %all_to_all.28.in_ref = bf16[8,88,128]{2,1,0:T(8,128)(2,1)S(1)} all-to-all(bf16[8,88,128]{2,1,0:T(8,128)(2,1)S(1)} %relay.1), channel_id=1, replica_groups=mesh['img_0'=4,'img_1'=4,'img_2'=2,'strip'=8] {'strip'}, dimensions={0} | all-to-all | bytes 360448 | tf_op jit(solution)/shard_map/all_to_all | solution.py:474
  112.2 2.2 %finish.1 = (bf16[32,128,128]{2,1,0:T(8,128)(2,1)}, f32[36,128]{1,0:T(8,128)}, f32[36,128]{1,0:T(8,128)}, f32[4,128]{1,0:T(4,128)}) custom-call(s32[1,1]{1,0:T(1,128)S(6)} %copy.13.len_ref, bf16[8,88,128]{2,1,0:T(8,128)(2,1)S(1)} %all_to_all.28.in_ref, f32[8,8,128]{2,1,0:T(8,128)S(1)} %all-to-all-done.st_ref.st1_ref, bf16[32,128,128]{2,1,0:T(8,128)(2,1)S(1)} %bitcast.11, ...), custom_call_target="tpu_custom_call" | custom-call | flops 6291456 | bytes 5242880 | tf_op jit(solution)/shard_map/finish/pallas_call | solution.py:583
Async XLA Ops:
  0.6 26.5 %copy-start.3 = (bf16[3,3,128,128]{3,2,1,0:T(8,128)(2,1)S(1)}, bf16[3,3,128,128]{3,2,1,0:T(8,128)(2,1)}, u32[]{:S(2)}) copy-start(bf16[3,3,128,128]{3,2,1,0:T(8,128)(2,1)} %first_ref.1) | copy-start | bytes 884740
  0.6 33.4 %copy-start.8 = (f32[128]{0:T(128)S(1)}, f32[128]{0:T(128)}, u32[]{:S(2)}) copy-start(f32[128]{0:T(128)} %param.14) | copy-start | bytes 1540
  0.7 33.4 %copy-start.6 = (f32[128]{0:T(128)S(1)}, f32[128]{0:T(128)}, u32[]{:S(2)}) copy-start(f32[128]{0:T(128)} %param.13) | copy-start | bytes 1540
  4.2 29.8 %collective-permute-start = (bf16[4,128,128]{2,1,0:T(8,128)(2,1)}, bf16[4,128,128]{2,1,0:T(8,128)(2,1)S(1)}, u32[]{:S(2)}, u32[]{:S(2)}) collective-permute-start(bf16[4,128,128]{2,1,0:T(8,128)(2,1)} %get-tuple-element.35), channel_id=1, source_target_pairs={{0,1},{1,2},{2,3},{3,4},{4,5},{5,6},{6,7},{8,9},{9,10},{10,11},{11... | collective-permute-start | bytes 393224 | tf_op jit(solution)/shard_map/ppermute | solution.py:480
  8.6 25.4 %collective-permute-start.1 = (bf16[4,128,128]{2,1,0:T(8,128)(2,1)}, bf16[4,128,128]{2,1,0:T(8,128)(2,1)S(1)}, u32[]{:S(2)}, u32[]{:S(2)}) collective-permute-start(bf16[4,128,128]{2,1,0:T(8,128)(2,1)} %get-tuple-element.36), channel_id=1, source_target_pairs={{1,0},{2,1},{3,2},{4,3},{5,4},{6,5},{7,6},{9,8},{10,9},{11,10},{12... | collective-permute-start | bytes 393224 | tf_op jit(solution)/shard_map/ppermute | solution.py:480
  9.9 24.1 %collective-permute-start.2 = (bf16[2,128,128]{2,1,0:T(8,128)(2,1)}, bf16[2,128,128]{2,1,0:T(8,128)(2,1)S(1)}, u32[]{:S(2)}, u32[]{:S(2)}) collective-permute-start(bf16[2,128,128]{2,1,0:T(8,128)(2,1)} %get-tuple-element.37), channel_id=1, source_target_pairs={{0,2},{1,3},{2,4},{3,5},{4,6},{5,7},{8,10},{9,11},{10,12},{11,13},... | collective-permute-start | bytes 196616 | tf_op jit(solution)/shard_map/ppermute | solution.py:480
  15.4 18.6 %collective-permute-start.3 = (bf16[2,128,128]{2,1,0:T(8,128)(2,1)}, bf16[2,128,128]{2,1,0:T(8,128)(2,1)S(1)}, u32[]{:S(2)}, u32[]{:S(2)}) collective-permute-start(bf16[2,128,128]{2,1,0:T(8,128)(2,1)} %get-tuple-element.38), channel_id=1, source_target_pairs={{2,0},{3,1},{4,2},{5,3},{6,4},{7,5},{10,8},{11,9},{12,10},{13,11},... | collective-permute-start | bytes 196616 | tf_op jit(solution)/shard_map/ppermute | solution.py:480
  16.7 17.3 %all-to-all-start = ((f32[8,8,128]{2,1,0:T(8,128)}), f32[8,8,128]{2,1,0:T(8,128)S(1)}, u32[]{:S(2)}, u32[]{:S(2)}) async-start(f32[8,8,128]{2,1,0:T(8,128)} %get-tuple-element.34), calls=%async_computation | async-start | bytes 65536 | tf_op jit(solution)/shard_map/all_to_all | solution.py:474
  27.2 1.0 copy-start.4
  34.1 1.2 %copy-start = (bf16[1,32,128,128]{3,2,1,0:T(8,128)(2,1)S(1)}, bf16[1,32,128,128]{3,2,1,0:T(8,128)(2,1)}, u32[]{:S(2)}) copy-start(bf16[1,32,128,128]{3,2,1,0:T(8,128)(2,1)} %param.9) | copy-start | bytes 3145732
  35.3 4.0 %copy-start.2 = (bf16[1,32,128,128]{3,2,1,0:T(8,128)(2,1)S(1)}, bf16[1,32,128,128]{3,2,1,0:T(8,128)(2,1)}, u32[]{:S(2)}) copy-start(bf16[1,32,128,128]{3,2,1,0:T(8,128)(2,1)} %param.10) | copy-start | bytes 3145732
  39.4 14.1 %copy-start.5 = (f32[128]{0:T(128)S(1)}, f32[128]{0:T(128)}, u32[]{:S(2)}) copy-start(f32[128]{0:T(128)} %param.15) | copy-start | bytes 1540
  39.4 14.1 %copy-start.7 = (f32[128]{0:T(128)S(1)}, f32[128]{0:T(128)}, u32[]{:S(2)}) copy-start(f32[128]{0:T(128)} %param.16) | copy-start | bytes 1540
  55.5 13.3 %copy-start.1 = (bf16[1,32,128,128]{3,2,1,0:T(8,128)(2,1)S(1)}, bf16[1,32,128,128]{3,2,1,0:T(8,128)(2,1)}, u32[]{:S(2)}) copy-start(bf16[1,32,128,128]{3,2,1,0:T(8,128)(2,1)} %param.9) | copy-start | bytes 3145732
where the time goes:
time: 115 us; the launch traced here: 114 us
  blocking collectives  55.4 us (48%)
  Pallas kernels  26.8 us (23%)
  starting transfers between devices  22.9 us (20%)
  waiting for transfers between devices  5.54 us (5%)
  local copies, waits for them, and re-layouts  2.21 us (2%)
  between operations  1.5 us (1%)
    all_to_all x4, blocking collectives, exchanged(): return lax.all_to_all(value, axis, split_axis=0, concat_axis=0, tiled=True)  55.4 us
    ppermute x4, starting transfers between devices, shifted(): return lax.ppermute(value, 'strip', pairs)  12.5 us
    all_to_all x1, starting transfers between devices, exchanged(): return lax.all_to_all(value, axis, split_axis=0, concat_axis=0, tiled=True)  10.4 us
    pallas_call x1, Pallas kernels, body(): call(dpre1_kernel, [SMEM, SMEM] + [VMEM] * 13, [shape((images, 2 * rows +...  6.41 us
    all_to_all x1, waiting for transfers between devices, exchanged(): return lax.all_to_all(value, axis, split_axis=0, concat_axis=0, tiled=True)  5.52 us
    pallas_call x1, Pallas kernels, body(): call(back_kernel, [SMEM, SMEM] + [VMEM] * 8, [shape((half + 2, COLS, PAIR...  4.84 us
    pallas_call x1, Pallas kernels, body(): call(hidden_kernel, [SMEM, SMEM] + [VMEM] * 9, [shape((SLOTS + 2, *edge),...  4.04 us
    pallas_call x1, Pallas kernels, body(): call(grad2_kernel, [SMEM] + [VMEM] * 2, [shape((WIDE, WIDE), F32)], flops...  4.01 us
  transfers between devices with their start and end apart: 5, of which 1 were waited for; matrix products, arithmetic and copies ran while one was open for 0% of the time, Pallas kernels for 0%

commit v1 on v0

v1 whole, which is shorter than its diff:
```python
import jax
import jax.numpy as jnp
from jax import lax
from jax.experimental import pallas as pl
from jax.experimental.pallas import tpu as pltpu
from jax.sharding import Mesh
from jax.sharding import PartitionSpec as P


IMG = ("img_0", "img_1", "img_2")
EPSILON = 1e-06
F32 = jnp.float32
BF16 = jnp.bfloat16
SLOTS = 32
COLS = 128
CH = 128
HEIGHT = 128
PER_GROUP = 4
PEERS = 8
CELLS = float(HEIGHT * COLS * PER_GROUP)
WIDE = 3 * CH
PAIR = 2 * WIDE
MIB = 1 << 20

VMEM = pl.BlockSpec(memory_space=pltpu.VMEM)
SMEM = pl.BlockSpec(memory_space=pltpu.SMEM)
HBM = pl.BlockSpec(memory_space=pltpu.HBM)


def shape(dims, dtype):
    return jax.ShapeDtypeStruct(dims, dtype)


def call(body, in_specs, outs, flops=0, moved=0, scratch=(), limit=12 * MIB, outs_in=None):
    return pl.pallas_call(
        body,
        in_specs=in_specs,
        out_specs=outs_in or [VMEM] * len(outs),
        out_shape=outs,
        scratch_shapes=scratch,
        compiler_params=pltpu.CompilerParams(vmem_limit_bytes=limit),
        cost_estimate=pl.CostEstimate(flops=flops, bytes_accessed=moved, transcendentals=0),
    )


def folded(row):
    lanes = jnp.broadcast_to(row, (8, CH))
    lane = lax.broadcasted_iota(jnp.int32, (8, CH), 1)
    lanes = lanes + jnp.where(lane % 2 == 0, pltpu.roll(lanes, CH - 1, 1), pltpu.roll(lanes, 1, 1))
    lanes = lanes + jnp.where(lane % 4 < 2, pltpu.roll(lanes, CH - 2, 1), pltpu.roll(lanes, 2, 1))
    return lanes[0:1]


def group_stats(stats):
    total = stats[0, 0:1]
    for j in range(1, PEERS):
        total = total + stats[j, 0:1]
    mean = folded(total) / CELLS
    spread = jnp.zeros((1, CH), F32)
    for j in range(PEERS):
        count = stats[j, 2:3] * float(COLS)
        gap = stats[j, 0:1] / count - mean
        spread = spread + stats[j, 1:2] + count * gap * gap
    return mean, lax.rsqrt(folded(spread) / CELLS + EPSILON)


def moments(sums, gain):
    cross, plain = sums[0, 0:1], sums[0, 1:2]
    for j in range(1, PEERS):
        cross, plain = cross + sums[j, 0:1], plain + sums[j, 1:2]
    return folded(cross * gain) / CELLS, folded(plain * gain) / CELLS


def sums8(value):
    return jnp.sum(value.reshape(-1, 8, value.shape[-1]), axis=0)


def send(out_ref, rows):
    index = lax.broadcasted_iota(jnp.int32, (8, CH), 0)
    tile = jnp.zeros((8, CH), F32)
    for k, row in enumerate(rows):
        tile = jnp.where(index == k, row, tile)
    for j in range(PEERS):
        out_ref[j] = tile


def channel_stats(load, length, out_ref):
    def first(i, acc):
        for k in range(4):
            r = i * 4 + k
            acc = acc + jnp.where(r < length, sums8(load(r)), 0.0)
        return acc

    total = jnp.sum(lax.fori_loop(0, SLOTS // 4, first, jnp.zeros((8, CH), F32)), axis=0, keepdims=True)
    used = length.astype(F32)
    mean = total / (used * float(COLS))

    def second(i, acc):
        for k in range(4):
            r = i * 4 + k
            gap = load(r) - mean
            acc = acc + jnp.where(r < length, sums8(gap * gap), 0.0)
        return acc

    spread = jnp.sum(lax.fori_loop(0, SLOTS // 4, second, jnp.zeros((8, CH), F32)), axis=0, keepdims=True)
    send(out_ref, [total, spread, jnp.broadcast_to(used, (1, CH))])


def sigmoid(z):
    return 0.5 * jnp.tanh(0.5 * z) + 0.5


def taps(row):
    col = lax.broadcasted_iota(jnp.int32, (COLS, CH), 0)
    before = jnp.where(col == 0, 0.0, pltpu.roll(row, 1, 0))
    after = jnp.where(col == COLS - 1, 0.0, pltpu.roll(row, COLS - 1, 0))
    return jnp.concatenate([before.astype(BF16), row.astype(BF16), after.astype(BF16)], axis=1)


def place_halo(buf, length, above, below):
    buf[0, :, 0:WIDE] = above
    pair = (length + 1) // 2

    @pl.when(length % 2 == 1)
    def _():
        buf[pair, :, 0:WIDE] = below

    @pl.when(length % 2 == 0)
    def _():
        buf[pair, :, WIDE:PAIR] = below


def fill_taps(buf, load):
    half = SLOTS // 2
    buf[half, :, WIDE:PAIR] = jnp.zeros((COLS, WIDE), BF16)

    def step(p, carry):
        buf[p, :, WIDE:PAIR] = taps(load(2 * p))
        buf[p + 1, :, 0:WIDE] = taps(load(2 * p + 1))
        return carry

    lax.fori_loop(0, half, step, 0)


def convolve(buf, w_ref, out_ref, chunk=8):
    for begin in range(0, SLOTS // 2, chunk):
        upper = buf[begin : begin + chunk].reshape(chunk * COLS, PAIR)
        lower = buf[begin + 1 : begin + 1 + chunk].reshape(chunk * COLS, PAIR)
        out = jnp.dot(upper, w_ref[0], preferred_element_type=F32)
        out = out + jnp.dot(lower, w_ref[1], preferred_element_type=F32)
        out = out.reshape(chunk, COLS, 2 * CH)
        for k in range(chunk):
            out_ref[2 * (begin + k)] = out[k, :, 0:CH]
            out_ref[2 * (begin + k) + 1] = out[k, :, CH:]


def transposed_taps(load, count, ahead, keep, out_ref):
    def step(p, carry):
        for k in range(2):
            i = 2 * p + k
            tile = load(p, k).T
            for tap in range(3):
                parity = (k + ahead - tap) % 2
                q = p + (k + ahead - tap - parity) // 2
                kept = jnp.where(keep(i, i + ahead - tap), tile, jnp.zeros_like(tile))
                lanes = pl.multiple_of((q + 1) * COLS, COLS)
                out_ref[parity, tap * CH : (tap + 1) * CH, pl.ds(lanes, COLS)] = kept
        return carry

    lax.fori_loop(0, count // 2, step, 0)


def kernel_grad(rows_t, even, odd):
    used = slice(COLS, COLS + even.shape[0] * COLS)
    grad = jnp.dot(rows_t[0, :, used], even.reshape(-1, WIDE), preferred_element_type=F32)
    return grad + jnp.dot(rows_t[1, :, used], odd.reshape(-1, WIDE), preferred_element_type=F32)


def stats_kernel(len_ref, x_ref, g_ref, top_ref, bottom_ref, out_ref, rows_ref, sem, edge_sem):
    length = len_ref[0, 0]
    last = length - 1
    whole = pltpu.make_async_copy(x_ref, rows_ref, sem)
    whole.start()
    started = []
    for k, ref in enumerate((x_ref, g_ref)):
        started.append(pltpu.make_async_copy(ref.at[0], top_ref.at[k], edge_sem.at[2 * k]))
        started.append(pltpu.make_async_copy(ref.at[last], bottom_ref.at[k], edge_sem.at[2 * k + 1]))
    for copy in started:
        copy.start()
    whole.wait()
    channel_stats(lambda r: rows_ref[r].astype(F32), length, out_ref)
    for copy in started:
        copy.wait()


def weights_kernel(first_ref, second_ref, ahead_ref, turned1_ref, turned2_ref):
    for out_ref in (ahead_ref, turned1_ref, turned2_ref):
        out_ref[0, WIDE * 0 : WIDE, CH : 2 * CH] = jnp.zeros((WIDE, CH), BF16)
        out_ref[1, WIDE:PAIR, 0:CH] = jnp.zeros((WIDE, CH), BF16)
    for a in range(3):
        for b in range(3):
            for v in range(2):
                half, lane = divmod((a + v) * WIDE + b * CH, PAIR)
                ahead_ref[half, lane : lane + CH, v * CH : (v + 1) * CH] = first_ref[a, b]
            for w_ref, out_ref in ((first_ref, turned1_ref), (second_ref, turned2_ref)):
                tile = w_ref[2 - a, 2 - b].T
                for v in range(2):
                    half, lane = divmod((a + v) * WIDE + b * CH, PAIR)
                    out_ref[half, lane : lane + CH, v * CH : (v + 1) * CH] = tile


def hidden_kernel(
    len_ref, strip_ref, x_ref, up_ref, down_ref, st_ref, w_ref, gain_ref, shift_ref, hid_ref, act_ref, out_ref
):
    length, strip = len_ref[0, 0], strip_ref[0]
    mean, inv = group_stats(st_ref)
    scale, shift = inv * gain_ref[...], shift_ref[...]

    def act(row):
        pre = (row.astype(F32) - mean) * scale + shift
        return pre * sigmoid(pre)

    fill_taps(act_ref, lambda r: act(x_ref[r]))
    place_halo(
        act_ref,
        length,
        taps(jnp.where(strip > 0, act(up_ref[0]), 0.0)),
        taps(jnp.where(strip < PEERS - 1, act(down_ref[0]), 0.0)),
    )
    convolve(act_ref, w_ref, hid_ref)
    channel_stats(lambda r: hid_ref[r], length, out_ref)


def back_kernel(len_ref, strip_ref, g_ref, up_ref, down_ref, w_ref, act_ref, g_taps_ref, back_ref, act_t_ref):
    length, strip = len_ref[0, 0], strip_ref[0]
    fill_taps(g_taps_ref, lambda r: g_ref[r].astype(F32))
    place_halo(
        g_taps_ref,
        length,
        taps(jnp.where(strip > 0, up_ref[1].astype(F32), 0.0)),
        taps(jnp.where(strip < PEERS - 1, down_ref[1].astype(F32), 0.0)),
    )
    convolve(g_taps_ref, w_ref, back_ref)
    transposed_taps(
        lambda p, k: act_ref[p, :, k * WIDE + CH : k * WIDE + 2 * CH],
        SLOTS + 2,
        0,
        lambda i, o: (o >= 0) & (o < length),
        act_t_ref,
    )


def dpre2_kernel(
    len_ref, st_ref, hid_ref, back_ref, gain_ref, shift_ref, act_ref, dpre_ref, top_ref, bottom_ref, out_ref
):
    length = len_ref[0, 0]
    mean, inv = group_stats(st_ref)
    gain, shift = gain_ref[...], shift_ref[...]

    def step(i, carry):
        cross, plain = carry
        for k in range(2):
            r = 2 * i + k
            normed = (hid_ref[r] - mean) * inv
            pre = normed * gain + shift
            s = sigmoid(pre)
            act = pre * s
            act_ref[r] = act.astype(BF16)
            grad = jnp.where(r < length, back_ref[r] * (s + act * (1.0 - s)), 0.0)
            dpre_ref[r] = grad
            plain = plain + sums8(grad)
            cross = cross + sums8(grad * normed)
        return cross, plain

    zero = jnp.zeros((8, CH), F32)
    cross, plain = lax.fori_loop(0, SLOTS // 2, step, (zero, zero))
    send(out_ref, [jnp.sum(cross, axis=0, keepdims=True), jnp.sum(plain, axis=0, keepdims=True)])
    for ref, row in ((top_ref, 0), (bottom_ref, length - 1)):
        ref[0] = dpre_ref[row]
        ref[1] = hid_ref[row]


def grad2_kernel(len_ref, act_ref, g_taps_ref, out_ref, act_t_ref):
    length = len_ref[0, 0]
    half = SLOTS // 2
    for tap, o in ((0, 0), (0, 1), (1, 0), (1, SLOTS + 1), (2, SLOTS), (2, SLOTS + 1)):
        lanes = (o // 2 + 1) * COLS
        act_t_ref[o % 2, tap * CH : (tap + 1) * CH, lanes : lanes + COLS] = jnp.zeros((CH, COLS), BF16)
    transposed_taps(lambda p, k: act_ref[2 * p + k], SLOTS, 2, lambda i, o: i < length, act_t_ref)
    out_ref[...] = kernel_grad(
        act_t_ref, g_taps_ref[0 : half + 1, :, 0:WIDE], g_taps_ref[0 : half + 1, :, WIDE:PAIR]
    )


def dpre1_kernel(
    len_ref, strip_ref, st1_ref, st2_ref, sums_ref, own_sums_ref, hid_ref, dpre2_ref, up_ref, down_ref, act_t_ref,
    x_ref, grad2_ref, w_ref, gain1_ref, shift1_ref, gain2_ref,
    share_ref, dpre_ref, out_ref, d_taps_ref, grad1_ref,
):
    length, strip = len_ref[0, 0], strip_ref[0]
    half = SLOTS // 2
    mean2, inv2 = group_stats(st2_ref)
    gain2 = gain2_ref[...]
    cross2, plain2 = moments(sums_ref, gain2)

    def dhidden(dpre, hidden):
        return inv2 * (dpre * gain2 - plain2 - (hidden - mean2) * inv2 * cross2)

    fill_taps(d_taps_ref, lambda r: jnp.where(r < length, dhidden(dpre2_ref[r], hid_ref[r]), 0.0))
    place_halo(
        d_taps_ref,
        length,
        taps(jnp.where(strip > 0, dhidden(up_ref[0], up_ref[1]), 0.0)),
        taps(jnp.where(strip < PEERS - 1, dhidden(down_ref[0], down_ref[1]), 0.0)),
    )
    grad1_ref[...] = kernel_grad(act_t_ref, d_taps_ref[0:half, :, WIDE:PAIR], d_taps_ref[1 : half + 1, :, 0:WIDE])
    convolve(d_taps_ref, w_ref, dpre_ref)
    mean1, inv1 = group_stats(st1_ref)
    gain1, shift1 = gain1_ref[...], shift1_ref[...]

    def slope(i, carry):
        cross, plain = carry
        for k in range(2):
            r = 2 * i + k
            normed = (x_ref[r].astype(F32) - mean1) * inv1
            pre = normed * gain1 + shift1
            s = sigmoid(pre)
            grad = jnp.where(r < length, dpre_ref[r] * (s + pre * s * (1.0 - s)), 0.0)
            dpre_ref[r] = grad
            plain = plain + sums8(grad)
            cross = cross + sums8(grad * normed)
        return cross, plain

    zero = jnp.zeros((8, CH), F32)
    cross, plain = lax.fori_loop(0, half, slope, (zero, zero))
    cross, plain = jnp.sum(cross, axis=0, keepdims=True), jnp.sum(plain, axis=0, keepdims=True)
    index = lax.broadcasted_iota(jnp.int32, (8, CH), 0)
    norm = jnp.where(index == 0, cross, jnp.where(index == 1, plain, 0.0))
    out_ref[...] = norm
    norm = norm + jnp.where(index == 2, own_sums_ref[0, 0:1], 0.0) + jnp.where(index == 3, own_sums_ref[0, 1:2], 0.0)
    blocks, rows = share_ref.shape[0], (share_ref.shape[1] - 8) // 2
    for j in range(blocks):
        share_ref[j] = packed(cut(grad1_ref, j * rows, rows), cut(grad2_ref, j * rows, rows), norm)


def cut(ref, begin, count):
    pieces = []
    while count:
        tap, row = divmod(begin, CH)
        here = min(count, CH - row)
        a, b = divmod(tap, 3)
        pieces.append(ref[a * CH + row : a * CH + row + here, (2 - b) * CH : (3 - b) * CH])
        begin, count = begin + here, count - here
    return pieces


def packed(first, second, norm):
    high = norm.astype(BF16).astype(F32)
    return jnp.concatenate([*first, *second, high[0:4], (norm - high)[0:4]], axis=0).astype(BF16)


def unpacked(total):
    rows = (total.shape[0] - 8) // 2
    norm = total[2 * rows : 2 * rows + 4] + total[2 * rows + 4 :]
    return total[0:rows], total[rows : 2 * rows], norm


def relay_kernel(in_ref, own_ref, out_ref):
    total = in_ref[0].astype(F32)
    for j in range(1, in_ref.shape[0]):
        total = total + in_ref[j].astype(F32)
    first, second, norm = unpacked(total)
    norm = jnp.concatenate([norm, jnp.zeros((4, CH), F32)], axis=0)
    own = own_ref[...]
    high = own.astype(BF16).astype(F32)
    image = jnp.concatenate([high[0:4], (own - high)[0:4]], axis=0).astype(BF16)
    tile = jnp.concatenate([packed([first], [second], norm), image], axis=0)
    for j in range(PEERS):
        out_ref[j] = tile


def finish_kernel(
    len_ref, in_ref, st_ref, x_ref, g_ref, dpre_ref, gain_ref, image_ref, first_ref, second_ref, norm_ref
):
    total = in_ref[0].astype(F32)
    for j in range(1, PEERS):
        total = total + in_ref[j].astype(F32)
    rows = first_ref.shape[0]
    first_ref[...], second_ref[...], norm_ref[...] = unpacked(total[0 : 2 * rows + 8])
    sums = total[2 * rows + 8 : 2 * rows + 12] + total[2 * rows + 12 : 2 * rows + 16]
    length = len_ref[0, 0]
    mean, inv = group_stats(st_ref)
    gain = gain_ref[...]
    cross, plain = folded(sums[0:1] * gain) / CELLS, folded(sums[1:2] * gain) / CELLS

    def step(i, carry):
        for k in range(2):
            r = 2 * i + k
            normed = (x_ref[r].astype(F32) - mean) * inv
            grad = inv * (dpre_ref[r] * gain - plain - normed * cross)
            grad = jnp.where(r < length, g_ref[r].astype(F32) + grad, 0.0)
            image_ref[r] = grad.astype(BF16)
        return carry

    lax.fori_loop(0, SLOTS // 2, step, 0)


def exchanged(value, axis):
    return lax.all_to_all(value, axis, split_axis=0, concat_axis=0, tiled=True)


def shifted(value, by):
    return lax.ppermute(value, "strip", [(i, (i + by) % PEERS) for i in range(PEERS)])


def body(
    image_in, cotangent, conv1_w, conv2_w, norm1_gain, norm1_shift, norm2_gain, norm2_shift, strip_rows
):
    x, g = image_in[0], cotangent[0]
    gain1, shift1 = norm1_gain[None], norm1_shift[None]
    gain2, shift2 = norm2_gain[None], norm2_shift[None]
    strip = lax.axis_index("strip")
    strip_id = strip.reshape(1).astype(jnp.int32)
    images = lax.axis_size(IMG)
    half = SLOTS // 2
    field = SLOTS * COLS * CH
    conv_flops = 2 * 9 * field * CH
    edge = (COLS, CH)
    stat = shape((PEERS, 8, CH), F32)

    top, bottom, stats1 = call(
        stats_kernel,
        [SMEM, HBM, HBM],
        [shape((2, *edge), BF16), shape((2, *edge), BF16), stat],
        flops=field * 6,
        moved=field * 2,
        scratch=[pltpu.VMEM((SLOTS, *edge), BF16), pltpu.SemaphoreType.DMA, pltpu.SemaphoreType.DMA((4,))],
        limit=63 * MIB + MIB // 2,
    )(strip_rows, x, g)
    up, down = shifted(bottom, 1), shifted(top, -1)
    weights1, turned1, turned2 = call(
        weights_kernel, [VMEM, VMEM], [shape((2, PAIR, 2 * CH), BF16)] * 3, flops=field * 2, moved=field
    )(conv1_w, conv2_w)
    stats1 = exchanged(stats1, "strip")

    hidden, act1, stats2 = call(
        hidden_kernel,
        [SMEM, SMEM] + [VMEM] * 7,
        [shape((SLOTS, *edge), F32), shape((half + 1, COLS, PAIR), BF16), stat],
        flops=conv_flops,
        moved=field * 6,
    )(strip_rows, strip_id, x, up, down, stats1, weights1, gain1, shift1)

    g_taps, back2, act1_t = call(
        back_kernel,
        [SMEM, SMEM] + [VMEM] * 5,
        [
            shape((half + 1, COLS, PAIR), BF16),
            shape((SLOTS, *edge), F32),
            shape((2, WIDE, (half + 2) * COLS), BF16),
        ],
        flops=conv_flops,
        moved=field * 6,
    )(strip_rows, strip_id, g, up, down, turned2, act1)
    stats2, g_taps, back2, act1_t = lax.optimization_barrier((stats2, g_taps, back2, act1_t))
    stats2 = exchanged(stats2, "strip")

    act2, dpre2, top, bottom, own_sums2 = call(
        dpre2_kernel,
        [SMEM] + [VMEM] * 5,
        [
            shape((SLOTS, *edge), BF16), shape((SLOTS, *edge), F32), shape((2, *edge), F32), shape((2, *edge), F32), stat,
        ],
        flops=field * 40,
        moved=field * 8,
    )(strip_rows, stats2, hidden, back2, gain2, shift2)
    up, down = shifted(bottom, 1), shifted(top, -1)

    (grad2,) = call(
        grad2_kernel,
        [SMEM] + [VMEM] * 2,
        [shape((WIDE, WIDE), F32)],
        flops=conv_flops,
        moved=field * 6,
        scratch=[pltpu.VMEM((2, WIDE, (half + 2) * COLS), BF16)],
    )(strip_rows, act2, g_taps)
    own_sums2, grad2, up, down = lax.optimization_barrier((own_sums2, grad2, up, down))
    sums2 = exchanged(own_sums2, "strip")

    rows = 9 * CH // images
    share, dpre1, own_sums1 = call(
        dpre1_kernel,
        [SMEM, SMEM] + [VMEM] * 15,
        [shape((images, 2 * rows + 8, CH), BF16), shape((SLOTS, *edge), F32), shape((8, CH), F32)],
        flops=2 * conv_flops,
        moved=field * 8,
        scratch=[pltpu.VMEM((half + 1, COLS, PAIR), BF16), pltpu.VMEM((WIDE, WIDE), F32)],
    )(
        strip_rows, strip_id, stats1, stats2, sums2, own_sums2, hidden, dpre2, up, down, act1_t, x, grad2, turned1,
        gain1, shift1, gain2,
    )
    share, dpre1, own_sums1 = lax.optimization_barrier((share, dpre1, own_sums1))
    share = exchanged(share, IMG)
    (relayed,) = call(
        relay_kernel, [VMEM, VMEM], [shape((PEERS, 2 * rows + 16, CH), BF16)], moved=images * (2 * rows + 8) * CH * 2
    )(share, own_sums1)
    relayed = exchanged(relayed, "strip")
    image_grad, grad1, grad2, norm_grads = call(
        finish_kernel,
        [SMEM] + [VMEM] * 6,
        [shape((SLOTS, *edge), BF16), shape((rows, CH), F32), shape((rows, CH), F32), shape((4, CH), F32)],
        flops=field * 12,
        moved=field * 10,
    )(strip_rows, relayed, stats1, x, g, dpre1, gain1)
    return image_grad[None], grad1, grad2, norm_grads


def solution(mesh):
    torus = Mesh(mesh.devices.reshape(4, 4, 2, mesh.shape["strip"]), (*IMG, "strip"))
    return jax.shard_map(
        body,
        mesh=torus,
        in_specs=(
            P(IMG, "strip", None, None), P(IMG, "strip", None, None), P(), P(), P(), P(), P(), P(), P(IMG, "strip"),
        ),
        out_specs=(P(IMG, "strip", None, None), P(IMG, None), P(IMG, None), P()),
        check_vma=False,
    )
```

time: 115 us -> 105 us (0.913)
  starting transfers between devices: 22.9 us -> 14.5 us
  Pallas kernels: 26.8 us -> 24.5 us
  blocking collectives: 55.4 us -> 56.8 us
    all_to_all x1, starting transfers between devices: 10.4 us -> 5.2 us  [exchanged(): return lax.all_to_all(value, axis, split_axis=0, concat_axis=0, tiled=True)]
    ppermute x4, starting transfers between devices: 12.5 us -> 9.31 us  [shifted(): lax.ppermute(value, 'strip', [(i, (i + by) % PEERS) for i in range(PEERS)])]
    pallas_call x5, Pallas kernels: 20.1 us -> 18.4 us  [the longest x1 6.34 us: body(): call(dpre1_kernel, [SMEM, SMEM] + [VMEM] * 15, [shape((images, 2 * rows +...]
    all_to_all x4, blocking collectives: 55.4 us -> 56.8 us  [exchanged(): return lax.all_to_all(value, axis, split_axis=0, concat_axis=0, tiled=True)]
  transfers between devices with their start and end apart: 5 -> 5, of which waited for: 1 -> 1; matrix products, arithmetic and copies ran while one was open for 0% -> 0% of each run, Pallas kernels for 0% -> 4%
where the time goes in v1:
time: 105 us
  blocking collectives  56.8 us (54%)
  Pallas kernels  24.5 us (23%)
  starting transfers between devices  14.5 us (14%)
  waiting for transfers between devices  5.59 us (5%)
  local copies, waits for them, and re-layouts  2.21 us (2%)
  between operations  1.47 us (1%)
    all_to_all x4, blocking collectives, exchanged(): return lax.all_to_all(value, axis, split_axis=0, concat_axis=0, tiled=True)  56.8 us
    ppermute x4, starting transfers between devices, shifted(): lax.ppermute(value, 'strip', [(i, (i + by) % PEERS) for i in range(PEERS)])  9.31 us
    pallas_call x1, Pallas kernels, body(): call(dpre1_kernel, [SMEM, SMEM] + [VMEM] * 15, [shape((images, 2 * rows +...  6.34 us
    all_to_all x1, waiting for transfers between devices, exchanged(): return lax.all_to_all(value, axis, split_axis=0, concat_axis=0, tiled=True)  5.58 us
    all_to_all x1, starting transfers between devices, exchanged(): return lax.all_to_all(value, axis, split_axis=0, concat_axis=0, tiled=True)  5.2 us
    pallas_call x1, Pallas kernels, body(): call(back_kernel, [SMEM, SMEM] + [VMEM] * 5, [shape((half + 1, COLS, PAIR...  4 us
    pallas_call x1, Pallas kernels, body(): call(hidden_kernel, [SMEM, SMEM] + [VMEM] * 7, [shape((SLOTS, *edge), F32...  3.83 us
    pallas_call x1, Pallas kernels, body(): call(grad2_kernel, [SMEM] + [VMEM] * 2, [shape((WIDE, WIDE), F32)], flops...  3.42 us
  transfers between devices with their start and end apart: 5, of which 1 were waited for; matrix products, arithmetic and copies ran while one was open for 0% of the time, Pallas kernels for 4%

profile of v1, /device:TPU:1, one launch (start us, length us, event | category | flops | bytes accessed | tf_op | source)
XLA Modules:
  0.0 105.1 jit_solution(854255149021700739)
XLA Ops:
  0.6 0.0 copy-start.3
  0.6 0.0 copy-start.8
  0.7 0.0 copy-start.6
  1.3 2.6 %shard_map.120 = (bf16[2,128,128]{2,1,0:T(8,128)(2,1)}, bf16[2,128,128]{2,1,0:T(8,128)(2,1)}, f32[8,8,128]{2,1,0:T(8,128)}) custom-call(s32[1,1]{1,0:T(1,128)S(6)} %copy.13.len_ref, bf16[32,128,128]{2,1,0:T(8,128)(2,1)} %bitcast.8, bf16[32,128,128]{2,1,0:T(8,128)(2,1)} %bitcast.12), custom_call_target="tpu_custom_call" | custom-call | flops 3145728 | bytes 1048576 | tf_op jit(solution)/shard_map/pallas_call | solution.py:431
  3.9 2.5 %collective-permute-start = (bf16[2,128,128]{2,1,0:T(8,128)(2,1)}, bf16[2,128,128]{2,1,0:T(8,128)(2,1)S(1)}, u32[]{:S(2)}, u32[]{:S(2)}) collective-permute-start(bf16[2,128,128]{2,1,0:T(8,128)(2,1)} %get-tuple-element.37), channel_id=1, source_target_pairs={{0,1},{1,2},{2,3},{3,4},{4,5},{5,6},{6,7},{7,0},{8,9},{9,10},{10,1... | collective-permute-start | bytes 196616 | tf_op jit(solution)/shard_map/ppermute | solution.py:413
  6.5 4.0 %collective-permute-start.1 = (bf16[2,128,128]{2,1,0:T(8,128)(2,1)}, bf16[2,128,128]{2,1,0:T(8,128)(2,1)S(1)}, u32[]{:S(2)}, u32[]{:S(2)}) collective-permute-start(bf16[2,128,128]{2,1,0:T(8,128)(2,1)} %get-tuple-element.38), channel_id=1, source_target_pairs={{0,7},{1,0},{2,1},{3,2},{4,3},{5,4},{6,5},{7,6},{8,15},{9,8},{10,9... | collective-permute-start | bytes 196616 | tf_op jit(solution)/shard_map/ppermute | solution.py:413
  10.5 5.2 %all-to-all-start = ((f32[8,8,128]{2,1,0:T(8,128)}), f32[8,8,128]{2,1,0:T(8,128)S(1)}, u32[]{:S(2)}, u32[]{:S(2)}) async-start(f32[8,8,128]{2,1,0:T(8,128)} %get-tuple-element.36), calls=%async_computation | async-start | bytes 65536 | tf_op jit(solution)/shard_map/all_to_all | solution.py:409
  15.7 0.0 copy-done.3
  15.7 0.0 copy-start.4
  15.7 1.0 copy-done.4
  16.7 0.4 shard_map.121
  17.0 5.6 %all-to-all-done.st_ref.st1_ref = f32[8,8,128]{2,1,0:T(8,128)S(1)} async-done(((f32[8,8,128]{2,1,0:T(8,128)}), f32[8,8,128]{2,1,0:T(8,128)S(1)}, u32[]{:S(2)}, u32[]{:S(2)}) %all-to-all-start) | async-done | bytes 32800 | tf_op jit(solution)/shard_map/all_to_all | solution.py:409
  22.6 0.0 collective-permute-done.up_ref
  22.6 0.0 collective-permute-done.1.down_ref
  22.6 0.0 copy-done.8
  22.6 0.0 copy-done.6
  22.6 0.0 copy-start
  22.6 1.2 %copy-done = bf16[1,32,128,128]{3,2,1,0:T(8,128)(2,1)S(1)} copy-done((bf16[1,32,128,128]{3,2,1,0:T(8,128)(2,1)S(1)}, bf16[1,32,128,128]{3,2,1,0:T(8,128)(2,1)}, u32[]{:S(2)}) %copy-start) | copy-done | bytes 1048600
  23.9 0.0 copy-start.2
  23.9 3.8 %shard_map.122 = (f32[32,128,128]{2,1,0:T(8,128)S(1)}, bf16[17,128,768]{2,1,0:T(8,128)(2,1)S(1)}, f32[8,8,128]{2,1,0:T(8,128)S(1)}) custom-call(s32[1,1]{1,0:T(1,128)S(6)} %copy.13.len_ref, s32[1]{0:T(128)} %bitcast.strip_ref, bf16[32,128,128]{2,1,0:T(8,128)(2,1)S(1)} %bitcast.9, bf16[2,128,128]{2,1,0:T(8,128)(2,1)S(1)} %collective-permute-done.up_ref, ...), custom_call_target="tpu_custom_call" | custom-call | flops 1207959552 | bytes 3145728 | tf_op jit(solution)/shard_map/pallas_call | solution.py:446
  27.7 0.0 copy-done.2
  27.7 0.0 copy-start.5
  27.7 0.0 copy-start.7
  27.7 4.0 %shard_map.123 = (bf16[17,128,768]{2,1,0:T(8,128)(2,1)S(1)}, f32[32,128,128]{2,1,0:T(8,128)S(1)}, bf16[2,384,2304]{2,1,0:T(8,128)(2,1)S(1)}) custom-call(s32[1,1]{1,0:T(1,128)S(6)} %copy.13.len_ref, s32[1]{0:T(128)} %bitcast.strip_ref, bf16[32,128,128]{2,1,0:T(8,128)(2,1)S(1)} %bitcast.13, bf16[2,128,128]{2,1,0:T(8,128)(2,1)S(1)} %collective-permute-done.up_ref, ...), custom_call_target="tpu_custom_call" | custom-call | flops 1207959552 | bytes 3145728 | tf_op jit(solution)/shard_map/pallas_call | solution.py:454
  31.7 9.2 %all_to_all.25.st_ref.st2_ref = f32[8,8,128]{2,1,0:T(8,128)S(1)} all-to-all(f32[8,8,128]{2,1,0:T(8,128)S(1)} %get-tuple-element.46), channel_id=1, replica_groups=mesh['img_0'=4,'img_1'=4,'img_2'=2,'strip'=8] {'strip'}, dimensions={0} | all-to-all | bytes 65536 | tf_op jit(solution)/shard_map/all_to_all | solution.py:409
  41.0 0.0 copy-done.5
  41.0 0.0 copy-done.7
  41.0 1.7 %shard_map.124 = (bf16[32,128,128]{2,1,0:T(8,128)(2,1)S(1)}, f32[32,128,128]{2,1,0:T(8,128)S(1)}, f32[2,128,128]{2,1,0:T(8,128)S(1)}, f32[2,128,128]{2,1,0:T(8,128)S(1)}, f32[8,8,128]{2,1,0:T(8,128)S(1)}) custom-call(s32[1,1]{1,0:T(1,128)S(6)} %copy.13.len_ref, f32[8,8,128]{2,1,0:T(8,128)S(1)} %all_to_all.25.st_ref.st2_ref, ...), custom_call_target="tpu_custom_call" | custom-call | flops 20971520 | bytes 4194304 | tf_op jit(solution)/shard_map/pallas_call | solution.py:468
  42.7 0.4 collective-permute-start.2
  43.0 2.4 %collective-permute-start.3 = (f32[2,128,128]{2,1,0:T(8,128)S(1)}, f32[2,128,128]{2,1,0:T(8,128)S(1)}, u32[]{:S(2)}, u32[]{:S(2)}) collective-permute-start(f32[2,128,128]{2,1,0:T(8,128)S(1)} %get-tuple-element.53), channel_id=1, source_target_pairs={{0,7},{1,0},{2,1},{3,2},{4,3},{5,4},{6,5},{7,6},{8,15},{9,8},{10,9... | collective-permute-start | bytes 393224 | tf_op jit(solution)/shard_map/ppermute | solution.py:413
  45.4 0.0 copy-start.1
  45.4 3.4 %shard_map.125.grad2_ref = f32[384,384]{1,0:T(8,128)S(1)} custom-call(s32[1,1]{1,0:T(1,128)S(6)} %copy.13.len_ref, bf16[32,128,128]{2,1,0:T(8,128)(2,1)S(1)} %get-tuple-element.50.act_ref, bf16[17,128,768]{2,1,0:T(8,128)(2,1)S(1)} %get-tuple-element.51.g_taps_ref), custom_call_target="tpu_custom_call" | custom-call | flops 1207959552 | bytes 3145728 | tf_op jit(solution)/shard_map/pallas_call | solution.py:479
  48.9 0.0 collective-permute-done.2.up_ref
  48.9 0.0 collective-permute-done.3.down_ref
  48.9 9.5 %all_to_all.26.sums_ref = f32[8,8,128]{2,1,0:T(8,128)S(1)} all-to-all(f32[8,8,128]{2,1,0:T(8,128)S(1)} %get-tuple-element.54.own_sums_ref), channel_id=1, replica_groups=mesh['img_0'=4,'img_1'=4,'img_2'=2,'strip'=8] {'strip'}, dimensions={0} | all-to-all | bytes 65536 | tf_op jit(solution)/shard_map/all_to_all | solution.py:409
  58.4 0.0 copy-done.1
  58.4 6.3 %shard_map.126 = (bf16[32,80,128]{2,1,0:T(8,128)(2,1)S(1)}, f32[32,128,128]{2,1,0:T(8,128)S(1)}, f32[8,128]{1,0:T(8,128)S(1)}) custom-call(s32[1,1]{1,0:T(1,128)S(6)} %copy.13.len_ref, s32[1]{0:T(128)} %bitcast.strip_ref, f32[8,8,128]{2,1,0:T(8,128)S(1)} %all-to-all-done.st_ref.st1_ref, f32[8,8,128]{2,1,0:T(8,128)S(1)} %all_to_all.25.st_ref.st2_ref, ...), custom_call_target="tpu_custom_call" | custom-call | flops 2415919104 | bytes 4194304 | tf_op jit(solution)/shard_map/pallas_call | solution.py:491
  64.7 26.4 %all_to_all.27.in_ref = bf16[32,80,128]{2,1,0:T(8,128)(2,1)S(1)} all-to-all(bf16[32,80,128]{2,1,0:T(8,128)(2,1)S(1)} %get-tuple-element.61), channel_id=1, replica_groups=mesh['img_0'=4,'img_1'=4,'img_2'=2,'strip'=8] {'img_0','img_1','img_2'}, dimensions={0} | all-to-all | bytes 1310720 | tf_op jit(solution)/shard_map/all_to_all | solution.py:409
  91.1 0.1 shard_map.127
  91.2 11.7 %all_to_all.28.in_ref = bf16[8,88,128]{2,1,0:T(8,128)(2,1)S(1)} all-to-all(bf16[8,88,128]{2,1,0:T(8,128)(2,1)S(1)} %shard_map.127), channel_id=1, replica_groups=mesh['img_0'=4,'img_1'=4,'img_2'=2,'strip'=8] {'strip'}, dimensions={0} | all-to-all | bytes 360448 | tf_op jit(solution)/shard_map/all_to_all | solution.py:409
  102.9 2.2 %shard_map.128 = (bf16[32,128,128]{2,1,0:T(8,128)(2,1)}, f32[36,128]{1,0:T(8,128)}, f32[36,128]{1,0:T(8,128)}, f32[4,128]{1,0:T(4,128)}) custom-call(s32[1,1]{1,0:T(1,128)S(6)} %copy.13.len_ref, bf16[8,88,128]{2,1,0:T(8,128)(2,1)S(1)} %all_to_all.28.in_ref, f32[8,8,128]{2,1,0:T(8,128)S(1)} %all-to-all-done.st_ref.st1_ref, ...), custom_call_target="tpu_custom_call" | custom-call | flops 6291456 | bytes 5242880 | tf_op jit(solution)/shard_map/pallas_call | solution.py:508
Async XLA Ops:
  0.6 15.1 %copy-start.3 = (bf16[3,3,128,128]{3,2,1,0:T(8,128)(2,1)S(1)}, bf16[3,3,128,128]{3,2,1,0:T(8,128)(2,1)}, u32[]{:S(2)}) copy-start(bf16[3,3,128,128]{3,2,1,0:T(8,128)(2,1)} %first_ref.1) | copy-start | bytes 884740
  0.6 22.0 %copy-start.8 = (f32[128]{0:T(128)S(1)}, f32[128]{0:T(128)}, u32[]{:S(2)}) copy-start(f32[128]{0:T(128)} %param.14) | copy-start | bytes 1540
  0.7 22.0 %copy-start.6 = (f32[128]{0:T(128)S(1)}, f32[128]{0:T(128)}, u32[]{:S(2)}) copy-start(f32[128]{0:T(128)} %param.13) | copy-start | bytes 1540
  3.9 18.7 %collective-permute-start = (bf16[2,128,128]{2,1,0:T(8,128)(2,1)}, bf16[2,128,128]{2,1,0:T(8,128)(2,1)S(1)}, u32[]{:S(2)}, u32[]{:S(2)}) collective-permute-start(bf16[2,128,128]{2,1,0:T(8,128)(2,1)} %get-tuple-element.37), channel_id=1, source_target_pairs={{0,1},{1,2},{2,3},{3,4},{4,5},{5,6},{6,7},{7,0},{8,9},{9,10},{10,1... | collective-permute-start | bytes 196616 | tf_op jit(solution)/shard_map/ppermute | solution.py:413
  6.5 16.1 %collective-permute-start.1 = (bf16[2,128,128]{2,1,0:T(8,128)(2,1)}, bf16[2,128,128]{2,1,0:T(8,128)(2,1)S(1)}, u32[]{:S(2)}, u32[]{:S(2)}) collective-permute-start(bf16[2,128,128]{2,1,0:T(8,128)(2,1)} %get-tuple-element.38), channel_id=1, source_target_pairs={{0,7},{1,0},{2,1},{3,2},{4,3},{5,4},{6,5},{7,6},{8,15},{9,8},{10,9... | collective-permute-start | bytes 196616 | tf_op jit(solution)/shard_map/ppermute | solution.py:413
  10.5 12.1 %all-to-all-start = ((f32[8,8,128]{2,1,0:T(8,128)}), f32[8,8,128]{2,1,0:T(8,128)S(1)}, u32[]{:S(2)}, u32[]{:S(2)}) async-start(f32[8,8,128]{2,1,0:T(8,128)} %get-tuple-element.36), calls=%async_computation | async-start | bytes 65536 | tf_op jit(solution)/shard_map/all_to_all | solution.py:409
  15.7 1.0 copy-start.4
  22.6 1.2 %copy-start = (bf16[1,32,128,128]{3,2,1,0:T(8,128)(2,1)S(1)}, bf16[1,32,128,128]{3,2,1,0:T(8,128)(2,1)}, u32[]{:S(2)}) copy-start(bf16[1,32,128,128]{3,2,1,0:T(8,128)(2,1)} %param.9) | copy-start | bytes 3145732
  23.9 3.8 %copy-start.2 = (bf16[1,32,128,128]{3,2,1,0:T(8,128)(2,1)S(1)}, bf16[1,32,128,128]{3,2,1,0:T(8,128)(2,1)}, u32[]{:S(2)}) copy-start(bf16[1,32,128,128]{3,2,1,0:T(8,128)(2,1)} %param.10) | copy-start | bytes 3145732
  27.7 13.3 %copy-start.5 = (f32[128]{0:T(128)S(1)}, f32[128]{0:T(128)}, u32[]{:S(2)}) copy-start(f32[128]{0:T(128)} %param.15) | copy-start | bytes 1540
  27.7 13.3 %copy-start.7 = (f32[128]{0:T(128)S(1)}, f32[128]{0:T(128)}, u32[]{:S(2)}) copy-start(f32[128]{0:T(128)} %param.16) | copy-start | bytes 1540
  42.7 6.2 %collective-permute-start.2 = (f32[2,128,128]{2,1,0:T(8,128)S(1)}, f32[2,128,128]{2,1,0:T(8,128)S(1)}, u32[]{:S(2)}, u32[]{:S(2)}) collective-permute-start(f32[2,128,128]{2,1,0:T(8,128)S(1)} %get-tuple-element.52), channel_id=1, source_target_pairs={{0,1},{1,2},{2,3},{3,4},{4,5},{5,6},{6,7},{7,0},{8,9},{9,10},{10,1... | collective-permute-start | bytes 393224 | tf_op jit(solution)/shard_map/ppermute | solution.py:413
  43.0 5.8 %collective-permute-start.3 = (f32[2,128,128]{2,1,0:T(8,128)S(1)}, f32[2,128,128]{2,1,0:T(8,128)S(1)}, u32[]{:S(2)}, u32[]{:S(2)}) collective-permute-start(f32[2,128,128]{2,1,0:T(8,128)S(1)} %get-tuple-element.53), channel_id=1, source_target_pairs={{0,7},{1,0},{2,1},{3,2},{4,3},{5,4},{6,5},{7,6},{8,15},{9,8},{10,9... | collective-permute-start | bytes 393224 | tf_op jit(solution)/shard_map/ppermute | solution.py:413
  45.4 13.0 %copy-start.1 = (bf16[1,32,128,128]{3,2,1,0:T(8,128)(2,1)S(1)}, bf16[1,32,128,128]{3,2,1,0:T(8,128)(2,1)}, u32[]{:S(2)}) copy-start(bf16[1,32,128,128]{3,2,1,0:T(8,128)(2,1)} %param.9) | copy-start | bytes 3145732

commit v2 on v1

--- a/solution.py
+++ b/solution.py
@@ -117,57 +117,45 @@
     return jnp.concatenate([before.astype(BF16), row.astype(BF16), after.astype(BF16)], axis=1)
 
 
-def place_halo(buf, length, above, below):
-    buf[0, :, 0:WIDE] = above
-    pair = (length + 1) // 2
-
-    @pl.when(length % 2 == 1)
-    def _():
-        buf[pair, :, 0:WIDE] = below
-
-    @pl.when(length % 2 == 0)
-    def _():
-        buf[pair, :, WIDE:PAIR] = below
-
-
-def fill_taps(buf, load):
-    half = SLOTS // 2
-    buf[half, :, WIDE:PAIR] = jnp.zeros((COLS, WIDE), BF16)
-
-    def step(p, carry):
-        buf[p, :, WIDE:PAIR] = taps(load(2 * p))
-        buf[p + 1, :, 0:WIDE] = taps(load(2 * p + 1))
-        return carry
-
-    lax.fori_loop(0, half, step, 0)
-
-
-def convolve(buf, w_ref, out_ref, chunk=8):
+def convolve(buf, w_ref, row_at, finish, beside=lambda step: None, chunk=4):
+    built = 0
     for begin in range(0, SLOTS // 2, chunk):
+        needed = 2 * (begin + chunk) + 2
+        for t in range(built, needed):
+            buf[t // 2, :, t % 2 * WIDE : (t % 2 + 1) * WIDE] = taps(row_at(t))
+        built = needed
+        beside(begin // chunk)
         upper = buf[begin : begin + chunk].reshape(chunk * COLS, PAIR)
         lower = buf[begin + 1 : begin + 1 + chunk].reshape(chunk * COLS, PAIR)
         out = jnp.dot(upper, w_ref[0], preferred_element_type=F32)
         out = out + jnp.dot(lower, w_ref[1], preferred_element_type=F32)
         out = out.reshape(chunk, COLS, 2 * CH)
         for k in range(chunk):
-            out_ref[2 * (begin + k)] = out[k, :, 0:CH]
-            out_ref[2 * (begin + k) + 1] = out[k, :, CH:]
-
-
-def transposed_taps(load, count, ahead, keep, out_ref):
-    def step(p, carry):
-        for k in range(2):
-            i = 2 * p + k
-            tile = load(p, k).T
-            for tap in range(3):
-                parity = (k + ahead - tap) % 2
-                q = p + (k + ahead - tap - parity) // 2
-                kept = jnp.where(keep(i, i + ahead - tap), tile, jnp.zeros_like(tile))
-                lanes = pl.multiple_of((q + 1) * COLS, COLS)
-                out_ref[parity, tap * CH : (tap + 1) * CH, pl.ds(lanes, COLS)] = kept
-        return carry
-
-    lax.fori_loop(0, count // 2, step, 0)
+            finish(2 * (begin + k), out[k, :, 0:CH])
+            finish(2 * (begin + k) + 1, out[k, :, CH:])
+
+
+def around(own, up, down, length, t):
+    if t == 0:
+        return up
+    if t == SLOTS + 1:
+        return down
+    return jnp.where(t <= length, own(t - 1), down)
+
+
+def in_image(length, strip, t):
+    if t == 0:
+        return strip > 0
+    return (t <= length) | (strip < PEERS - 1)
+
+
+def transposed_row(tile, i, ahead, keep, out_ref):
+    tile = tile.T
+    for tap in range(3):
+        o = i + ahead - tap
+        lanes = (o // 2 + 1) * COLS
+        kept = jnp.where(keep(o), tile, jnp.zeros_like(tile))
+        out_ref[o % 2, tap * CH : (tap + 1) * CH, lanes : lanes + COLS] = kept
 
 
 def kernel_grad(rows_t, even, odd):
@@ -216,38 +204,34 @@
     mean, inv = group_stats(st_ref)
     scale, shift = inv * gain_ref[...], shift_ref[...]
 
-    def act(row):
+    def row_at(t):
+        row = around(lambda r: x_ref[r], up_ref[0], down_ref[0], length, t)
         pre = (row.astype(F32) - mean) * scale + shift
-        return pre * sigmoid(pre)
-
-    fill_taps(act_ref, lambda r: act(x_ref[r]))
-    place_halo(
-        act_ref,
-        length,
-        taps(jnp.where(strip > 0, act(up_ref[0]), 0.0)),
-        taps(jnp.where(strip < PEERS - 1, act(down_ref[0]), 0.0)),
-    )
-    convolve(act_ref, w_ref, hid_ref)
+        return jnp.where(in_image(length, strip, t), pre * sigmoid(pre), 0.0)
+
+    def finish(r, row):
+        hid_ref[r] = row
+
+    convolve(act_ref, w_ref, row_at, finish)
     channel_stats(lambda r: hid_ref[r], length, out_ref)
 
 
 def back_kernel(len_ref, strip_ref, g_ref, up_ref, down_ref, w_ref, act_ref, g_taps_ref, back_ref, act_t_ref):
     length, strip = len_ref[0, 0], strip_ref[0]
-    fill_taps(g_taps_ref, lambda r: g_ref[r].astype(F32))
-    place_halo(
-        g_taps_ref,
-        length,
-        taps(jnp.where(strip > 0, up_ref[1].astype(F32), 0.0)),
-        taps(jnp.where(strip < PEERS - 1, down_ref[1].astype(F32), 0.0)),
-    )
-    convolve(g_taps_ref, w_ref, back_ref)
-    transposed_taps(
-        lambda p, k: act_ref[p, :, k * WIDE + CH : k * WIDE + 2 * CH],
-        SLOTS + 2,
-        0,
-        lambda i, o: (o >= 0) & (o < length),
-        act_t_ref,
-    )
+
+    def row_at(t):
+        row = around(lambda r: g_ref[r], up_ref[1], down_ref[1], length, t)
+        return jnp.where(in_image(length, strip, t), row.astype(F32), 0.0)
+
+    def finish(r, row):
+        back_ref[r] = row
+
+    def beside(step):
+        for i in range(step * 9, min(step * 9 + 9, SLOTS + 2)):
+            tile = act_ref[i // 2, :, i % 2 * WIDE + CH : i % 2 * WIDE + 2 * CH]
+            transposed_row(tile, i, 0, lambda o: (o >= 0) & (o < length), act_t_ref)
+
+    convolve(g_taps_ref, w_ref, row_at, finish, beside)
 
 
 def dpre2_kernel(
@@ -286,7 +270,8 @@
     for tap, o in ((0, 0), (0, 1), (1, 0), (1, SLOTS + 1), (2, SLOTS), (2, SLOTS + 1)):
         lanes = (o // 2 + 1) * COLS
         act_t_ref[o % 2, tap * CH : (tap + 1) * CH, lanes : lanes + COLS] = jnp.zeros((CH, COLS), BF16)
-    transposed_taps(lambda p, k: act_ref[2 * p + k], SLOTS, 2, lambda i, o: i < length, act_t_ref)
+    for i in range(SLOTS):
+        transposed_row(act_ref[i], i, 2, lambda o: i < length, act_t_ref)
     out_ref[...] = kernel_grad(
         act_t_ref, g_taps_ref[0 : half + 1, :, 0:WIDE], g_taps_ref[0 : half + 1, :, WIDE:PAIR]
     )
@@ -306,34 +291,27 @@
     def dhidden(dpre, hidden):
         return inv2 * (dpre * gain2 - plain2 - (hidden - mean2) * inv2 * cross2)
 
-    fill_taps(d_taps_ref, lambda r: jnp.where(r < length, dhidden(dpre2_ref[r], hid_ref[r]), 0.0))
-    place_halo(
-        d_taps_ref,
-        length,
-        taps(jnp.where(strip > 0, dhidden(up_ref[0], up_ref[1]), 0.0)),
-        taps(jnp.where(strip < PEERS - 1, dhidden(down_ref[0], down_ref[1]), 0.0)),
-    )
-    grad1_ref[...] = kernel_grad(act_t_ref, d_taps_ref[0:half, :, WIDE:PAIR], d_taps_ref[1 : half + 1, :, 0:WIDE])
-    convolve(d_taps_ref, w_ref, dpre_ref)
     mean1, inv1 = group_stats(st1_ref)
     gain1, shift1 = gain1_ref[...], shift1_ref[...]
-
-    def slope(i, carry):
-        cross, plain = carry
-        for k in range(2):
-            r = 2 * i + k
-            normed = (x_ref[r].astype(F32) - mean1) * inv1
-            pre = normed * gain1 + shift1
-            s = sigmoid(pre)
-            grad = jnp.where(r < length, dpre_ref[r] * (s + pre * s * (1.0 - s)), 0.0)
-            dpre_ref[r] = grad
-            plain = plain + sums8(grad)
-            cross = cross + sums8(grad * normed)
-        return cross, plain
-
-    zero = jnp.zeros((8, CH), F32)
-    cross, plain = lax.fori_loop(0, half, slope, (zero, zero))
-    cross, plain = jnp.sum(cross, axis=0, keepdims=True), jnp.sum(plain, axis=0, keepdims=True)
+    sums = [jnp.zeros((8, CH), F32), jnp.zeros((8, CH), F32)]
+
+    def row_at(t):
+        dpre = around(lambda r: dpre2_ref[r], up_ref[0], down_ref[0], length, t)
+        hidden = around(lambda r: hid_ref[r], up_ref[1], down_ref[1], length, t)
+        return jnp.where(in_image(length, strip, t), dhidden(dpre, hidden), 0.0)
+
+    def finish(r, row):
+        normed = (x_ref[r].astype(F32) - mean1) * inv1
+        pre = normed * gain1 + shift1
+        s = sigmoid(pre)
+        grad = jnp.where(r < length, row * (s + pre * s * (1.0 - s)), 0.0)
+        dpre_ref[r] = grad
+        sums[0] = sums[0] + sums8(grad * normed)
+        sums[1] = sums[1] + sums8(grad)
+
+    convolve(d_taps_ref, w_ref, row_at, finish)
+    grad1_ref[...] = kernel_grad(act_t_ref, d_taps_ref[0:half, :, WIDE:PAIR], d_taps_ref[1 : half + 1, :, 0:WIDE])
+    cross, plain = (jnp.sum(total, axis=0, keepdims=True) for total in sums)
     index = lax.broadcasted_iota(jnp.int32, (8, CH), 0)
     norm = jnp.where(index == 0, cross, jnp.where(index == 1, plain, 0.0))
     out_ref[...] = norm
@@ -435,7 +413,7 @@
         flops=field * 6,
         moved=field * 2,
         scratch=[pltpu.VMEM((SLOTS, *edge), BF16), pltpu.SemaphoreType.DMA, pltpu.SemaphoreType.DMA((4,))],
-        limit=63 * MIB + MIB // 2,
+        limit=63 * MIB + MIB // 4,
     )(strip_rows, x, g)
     up, down = shifted(bottom, 1), shifted(top, -1)
     weights1, turned1, turned2 = call(
@@ -484,7 +462,7 @@
         moved=field * 6,
         scratch=[pltpu.VMEM((2, WIDE, (half + 2) * COLS), BF16)],
     )(strip_rows, act2, g_taps)
-    own_sums2, grad2, up, down = lax.optimization_barrier((own_sums2, grad2, up, down))
+    own_sums2, grad2 = lax.optimization_barrier((own_sums2, grad2))
     sums2 = exchanged(own_sums2, "strip")
 
     rows = 9 * CH // images

time: 105 us -> 99.2 us (0.945)
  Pallas kernels: 24.5 us -> 19.6 us
  blocking collectives: 56.8 us -> 55.4 us
    pallas_call x1, Pallas kernels: 4 us -> 2.22 us  [body(): call(back_kernel, [SMEM, SMEM] + [VMEM] * 5, [shape((half + 1, COLS, PAIR...]
    pallas_call x1, Pallas kernels: 3.42 us -> 1.99 us  [body(): call(grad2_kernel, [SMEM] + [VMEM] * 2, [shape((WIDE, WIDE), F32)], flops...]
    all_to_all x4, blocking collectives: 56.8 us -> 55.4 us  [exchanged(): return lax.all_to_all(value, axis, split_axis=0, concat_axis=0, tiled=True)]
  transfers between devices with their start and end apart: 5 -> 5, of which waited for: 1 -> 1; matrix products, arithmetic and copies ran while one was open for 0% -> 0% of each run, Pallas kernels for 4% -> 2%
where the time goes in v2:
time: 99.2 us; the launch traced here: 98.8 us
  blocking collectives  55.4 us (56%)
  Pallas kernels  19.6 us (20%)
  starting transfers between devices  14.5 us (15%)
  waiting for transfers between devices  6.54 us (7%)
  between operations  1.48 us (1%)
  local copies, waits for them, and re-layouts  1.26 us (1%)
    all_to_all x4, blocking collectives, exchanged(): return lax.all_to_all(value, axis, split_axis=0, concat_axis=0, tiled=True)  55.4 us
    ppermute x4, starting transfers between devices, shifted(): lax.ppermute(value, 'strip', [(i, (i + by) % PEERS) for i in range(PEERS)])  9.31 us
    all_to_all x1, waiting for transfers between devices, exchanged(): return lax.all_to_all(value, axis, split_axis=0, concat_axis=0, tiled=True)  6.53 us
    pallas_call x1, Pallas kernels, body(): call(dpre1_kernel, [SMEM, SMEM] + [VMEM] * 15, [shape((images, 2 * rows +...  5.37 us
    all_to_all x1, starting transfers between devices, exchanged(): return lax.all_to_all(value, axis, split_axis=0, concat_axis=0, tiled=True)  5.2 us
    pallas_call x1, Pallas kernels, body(): call(hidden_kernel, [SMEM, SMEM] + [VMEM] * 7, [shape((SLOTS, *edge), F32...  3.16 us
    pallas_call x1, Pallas kernels, body(): call(stats_kernel, [SMEM, HBM, HBM], [shape((2, *edge), BF16), shape((2,...  2.57 us
    pallas_call x1, Pallas kernels, body(): call(back_kernel, [SMEM, SMEM] + [VMEM] * 5, [shape((half + 1, COLS, PAIR...  2.22 us
  transfers between devices with their start and end apart: 5, of which 1 were waited for; matrix products, arithmetic and copies ran while one was open for 0% of the time, Pallas kernels for 2%

profile of v2, /device:TPU:1, one launch (start us, length us, event | category | flops | bytes accessed | tf_op | source)
XLA Modules:
  0.0 98.8 jit_solution(6077280092176890372)
XLA Ops:
  0.6 0.0 copy-start.4
  0.6 0.0 copy-start.3
  0.7 0.0 copy-start.8
  0.7 0.0 copy-start.6
  1.4 2.6 %shard_map.120 = (bf16[2,128,128]{2,1,0:T(8,128)(2,1)}, bf16[2,128,128]{2,1,0:T(8,128)(2,1)}, f32[8,8,128]{2,1,0:T(8,128)}) custom-call(s32[1,1]{1,0:T(1,128)S(6)} %copy.13.len_ref, bf16[32,128,128]{2,1,0:T(8,128)(2,1)} %bitcast.8, bf16[32,128,128]{2,1,0:T(8,128)(2,1)} %bitcast.12), custom_call_target="tpu_custom_call" | custom-call | flops 3145728 | bytes 1048576 | tf_op jit(solution)/shard_map/pallas_call | solution.py:409
  4.0 2.5 %collective-permute-start = (bf16[2,128,128]{2,1,0:T(8,128)(2,1)}, bf16[2,128,128]{2,1,0:T(8,128)(2,1)S(1)}, u32[]{:S(2)}, u32[]{:S(2)}) collective-permute-start(bf16[2,128,128]{2,1,0:T(8,128)(2,1)} %get-tuple-element.35), channel_id=1, source_target_pairs={{0,1},{1,2},{2,3},{3,4},{4,5},{5,6},{6,7},{7,0},{8,9},{9,10},{10,1... | collective-permute-start | bytes 196616 | tf_op jit(solution)/shard_map/ppermute | solution.py:391
  6.5 4.0 %collective-permute-start.1 = (bf16[2,128,128]{2,1,0:T(8,128)(2,1)}, bf16[2,128,128]{2,1,0:T(8,128)(2,1)S(1)}, u32[]{:S(2)}, u32[]{:S(2)}) collective-permute-start(bf16[2,128,128]{2,1,0:T(8,128)(2,1)} %get-tuple-element.36), channel_id=1, source_target_pairs={{0,7},{1,0},{2,1},{3,2},{4,3},{5,4},{6,5},{7,6},{8,15},{9,8},{10,9... | collective-permute-start | bytes 196616 | tf_op jit(solution)/shard_map/ppermute | solution.py:391
  10.5 5.2 %all-to-all-start = ((f32[8,8,128]{2,1,0:T(8,128)}), f32[8,8,128]{2,1,0:T(8,128)S(1)}, u32[]{:S(2)}, u32[]{:S(2)}) async-start(f32[8,8,128]{2,1,0:T(8,128)} %get-tuple-element.34), calls=%async_computation | async-start | bytes 65536 | tf_op jit(solution)/shard_map/all_to_all | solution.py:387
  15.7 0.0 copy-done.4
  15.7 0.0 copy-done.3
  15.7 0.4 shard_map.121
  16.1 6.5 %all-to-all-done.st_ref.st1_ref = f32[8,8,128]{2,1,0:T(8,128)S(1)} async-done(((f32[8,8,128]{2,1,0:T(8,128)}), f32[8,8,128]{2,1,0:T(8,128)S(1)}, u32[]{:S(2)}, u32[]{:S(2)}) %all-to-all-start) | async-done | bytes 32800 | tf_op jit(solution)/shard_map/all_to_all | solution.py:387
  22.6 0.0 collective-permute-done.up_ref
  22.6 0.0 collective-permute-done.1.down_ref
  22.6 0.0 copy-done.8
  22.6 0.0 copy-done.6
  22.6 0.0 copy-start
  22.7 1.2 %copy-done = bf16[1,32,128,128]{3,2,1,0:T(8,128)(2,1)S(1)} copy-done((bf16[1,32,128,128]{3,2,1,0:T(8,128)(2,1)S(1)}, bf16[1,32,128,128]{3,2,1,0:T(8,128)(2,1)}, u32[]{:S(2)}) %copy-start) | copy-done | bytes 1048600
  23.9 0.0 copy-start.2
  23.9 3.2 %shard_map.122 = (f32[32,128,128]{2,1,0:T(8,128)S(1)}, bf16[17,128,768]{2,1,0:T(8,128)(2,1)S(1)}, f32[8,8,128]{2,1,0:T(8,128)S(1)}) custom-call(s32[1,1]{1,0:T(1,128)S(6)} %copy.13.len_ref, s32[1]{0:T(128)} %bitcast.strip_ref, bf16[32,128,128]{2,1,0:T(8,128)(2,1)S(1)} %bitcast.9, bf16[2,128,128]{2,1,0:T(8,128)(2,1)S(1)} %collective-permute-done.up_ref, ...), custom_call_target="tpu_custom_call" | custom-call | flops 1207959552 | bytes 3145728 | tf_op jit(solution)/shard_map/pallas_call | solution.py:424
  27.0 0.0 copy-done.2
  27.1 0.0 copy-start.5
  27.1 0.0 copy-start.7
  27.1 2.2 %shard_map.123 = (bf16[17,128,768]{2,1,0:T(8,128)(2,1)S(1)}, f32[32,128,128]{2,1,0:T(8,128)S(1)}, bf16[2,384,2304]{2,1,0:T(8,128)(2,1)S(1)}) custom-call(s32[1,1]{1,0:T(1,128)S(6)} %copy.13.len_ref, s32[1]{0:T(128)} %bitcast.strip_ref, bf16[32,128,128]{2,1,0:T(8,128)(2,1)S(1)} %bitcast.13, bf16[2,128,128]{2,1,0:T(8,128)(2,1)S(1)} %collective-permute-done.up_ref, ...), custom_call_target="tpu_custom_call" | custom-call | flops 1207959552 | bytes 3145728 | tf_op jit(solution)/shard_map/pallas_call | solution.py:432
  29.3 9.2 %all_to_all.25.st_ref.st2_ref = f32[8,8,128]{2,1,0:T(8,128)S(1)} all-to-all(f32[8,8,128]{2,1,0:T(8,128)S(1)} %get-tuple-element.44), channel_id=1, replica_groups=mesh['img_0'=4,'img_1'=4,'img_2'=2,'strip'=8] {'strip'}, dimensions={0} | all-to-all | bytes 65536 | tf_op jit(solution)/shard_map/all_to_all | solution.py:387
  38.5 0.0 copy-done.5
  38.6 0.0 copy-done.7
  38.6 1.7 %shard_map.124 = (bf16[32,128,128]{2,1,0:T(8,128)(2,1)S(1)}, f32[32,128,128]{2,1,0:T(8,128)S(1)}, f32[2,128,128]{2,1,0:T(8,128)S(1)}, f32[2,128,128]{2,1,0:T(8,128)S(1)}, f32[8,8,128]{2,1,0:T(8,128)S(1)}) custom-call(s32[1,1]{1,0:T(1,128)S(6)} %copy.13.len_ref, f32[8,8,128]{2,1,0:T(8,128)S(1)} %all_to_all.25.st_ref.st2_ref, ...), custom_call_target="tpu_custom_call" | custom-call | flops 20971520 | bytes 4194304 | tf_op jit(solution)/shard_map/pallas_call | solution.py:446
  40.3 0.4 collective-permute-start.2
  40.6 2.4 %collective-permute-start.3 = (f32[2,128,128]{2,1,0:T(8,128)S(1)}, f32[2,128,128]{2,1,0:T(8,128)S(1)}, u32[]{:S(2)}, u32[]{:S(2)}) collective-permute-start(f32[2,128,128]{2,1,0:T(8,128)S(1)} %get-tuple-element.53), channel_id=1, source_target_pairs={{0,7},{1,0},{2,1},{3,2},{4,3},{5,4},{6,5},{7,6},{8,15},{9,8},{10,9... | collective-permute-start | bytes 393224 | tf_op jit(solution)/shard_map/ppermute | solution.py:391
  43.0 0.0 copy-start.1
  43.0 2.0 %shard_map.125.grad2_ref = f32[384,384]{1,0:T(8,128)S(1)} custom-call(s32[1,1]{1,0:T(1,128)S(6)} %copy.13.len_ref, bf16[32,128,128]{2,1,0:T(8,128)(2,1)S(1)} %get-tuple-element.48.act_ref, bf16[17,128,768]{2,1,0:T(8,128)(2,1)S(1)} %get-tuple-element.49.g_taps_ref), custom_call_target="tpu_custom_call" | custom-call | flops 1207959552 | bytes 3145728 | tf_op jit(solution)/shard_map/pallas_call | solution.py:457
  45.0 9.2 %all_to_all.26.sums_ref = f32[8,8,128]{2,1,0:T(8,128)S(1)} all-to-all(f32[8,8,128]{2,1,0:T(8,128)S(1)} %get-tuple-element.50.own_sums_ref), channel_id=1, replica_groups=mesh['img_0'=4,'img_1'=4,'img_2'=2,'strip'=8] {'strip'}, dimensions={0} | all-to-all | bytes 65536 | tf_op jit(solution)/shard_map/all_to_all | solution.py:387
  54.2 0.0 collective-permute-done.2.up_ref
  54.2 0.0 collective-permute-done.3.down_ref
  54.2 0.0 copy-done.1
  54.3 5.4 %shard_map.126 = (bf16[32,80,128]{2,1,0:T(8,128)(2,1)S(1)}, f32[32,128,128]{2,1,0:T(8,128)S(1)}, f32[8,128]{1,0:T(8,128)S(1)}) custom-call(s32[1,1]{1,0:T(1,128)S(6)} %copy.13.len_ref, s32[1]{0:T(128)} %bitcast.strip_ref, f32[8,8,128]{2,1,0:T(8,128)S(1)} %all-to-all-done.st_ref.st1_ref, f32[8,8,128]{2,1,0:T(8,128)S(1)} %all_to_all.25.st_ref.st2_ref, ...), custom_call_target="tpu_custom_call" | custom-call | flops 2415919104 | bytes 4194304 | tf_op jit(solution)/shard_map/pallas_call | solution.py:469
  59.6 25.2 %all_to_all.27.in_ref = bf16[32,80,128]{2,1,0:T(8,128)(2,1)S(1)} all-to-all(bf16[32,80,128]{2,1,0:T(8,128)(2,1)S(1)} %get-tuple-element.57), channel_id=1, replica_groups=mesh['img_0'=4,'img_1'=4,'img_2'=2,'strip'=8] {'img_0','img_1','img_2'}, dimensions={0} | all-to-all | bytes 1310720 | tf_op jit(solution)/shard_map/all_to_all | solution.py:387
  84.9 0.1 shard_map.127
  85.0 11.7 %all_to_all.28.in_ref = bf16[8,88,128]{2,1,0:T(8,128)(2,1)S(1)} all-to-all(bf16[8,88,128]{2,1,0:T(8,128)(2,1)S(1)} %shard_map.127), channel_id=1, replica_groups=mesh['img_0'=4,'img_1'=4,'img_2'=2,'strip'=8] {'strip'}, dimensions={0} | all-to-all | bytes 360448 | tf_op jit(solution)/shard_map/all_to_all | solution.py:387
  96.6 2.2 %shard_map.128 = (bf16[32,128,128]{2,1,0:T(8,128)(2,1)}, f32[36,128]{1,0:T(8,128)}, f32[36,128]{1,0:T(8,128)}, f32[4,128]{1,0:T(4,128)}) custom-call(s32[1,1]{1,0:T(1,128)S(6)} %copy.13.len_ref, bf16[8,88,128]{2,1,0:T(8,128)(2,1)S(1)} %all_to_all.28.in_ref, f32[8,8,128]{2,1,0:T(8,128)S(1)} %all-to-all-done.st_ref.st1_ref, ...), custom_call_target="tpu_custom_call" | custom-call | flops 6291456 | bytes 5242880 | tf_op jit(solution)/shard_map/pallas_call | solution.py:486
Async XLA Ops:
  0.6 15.1 %copy-start.4 = (bf16[3,3,128,128]{3,2,1,0:T(8,128)(2,1)S(1)}, bf16[3,3,128,128]{3,2,1,0:T(8,128)(2,1)}, u32[]{:S(2)}) copy-start(bf16[3,3,128,128]{3,2,1,0:T(8,128)(2,1)} %second_ref.1) | copy-start | bytes 884740
  0.6 15.1 %copy-start.3 = (bf16[3,3,128,128]{3,2,1,0:T(8,128)(2,1)S(1)}, bf16[3,3,128,128]{3,2,1,0:T(8,128)(2,1)}, u32[]{:S(2)}) copy-start(bf16[3,3,128,128]{3,2,1,0:T(8,128)(2,1)} %first_ref.1) | copy-start | bytes 884740
  0.7 22.0 %copy-start.8 = (f32[128]{0:T(128)S(1)}, f32[128]{0:T(128)}, u32[]{:S(2)}) copy-start(f32[128]{0:T(128)} %param.14) | copy-start | bytes 1540
  0.7 22.0 %copy-start.6 = (f32[128]{0:T(128)S(1)}, f32[128]{0:T(128)}, u32[]{:S(2)}) copy-start(f32[128]{0:T(128)} %param.13) | copy-start | bytes 1540
  4.0 18.7 %collective-permute-start = (bf16[2,128,128]{2,1,0:T(8,128)(2,1)}, bf16[2,128,128]{2,1,0:T(8,128)(2,1)S(1)}, u32[]{:S(2)}, u32[]{:S(2)}) collective-permute-start(bf16[2,128,128]{2,1,0:T(8,128)(2,1)} %get-tuple-element.35), channel_id=1, source_target_pairs={{0,1},{1,2},{2,3},{3,4},{4,5},{5,6},{6,7},{7,0},{8,9},{9,10},{10,1... | collective-permute-start | bytes 196616 | tf_op jit(solution)/shard_map/ppermute | solution.py:391
  6.5 16.1 %collective-permute-start.1 = (bf16[2,128,128]{2,1,0:T(8,128)(2,1)}, bf16[2,128,128]{2,1,0:T(8,128)(2,1)S(1)}, u32[]{:S(2)}, u32[]{:S(2)}) collective-permute-start(bf16[2,128,128]{2,1,0:T(8,128)(2,1)} %get-tuple-element.36), channel_id=1, source_target_pairs={{0,7},{1,0},{2,1},{3,2},{4,3},{5,4},{6,5},{7,6},{8,15},{9,8},{10,9... | collective-permute-start | bytes 196616 | tf_op jit(solution)/shard_map/ppermute | solution.py:391
  10.5 12.1 %all-to-all-start = ((f32[8,8,128]{2,1,0:T(8,128)}), f32[8,8,128]{2,1,0:T(8,128)S(1)}, u32[]{:S(2)}, u32[]{:S(2)}) async-start(f32[8,8,128]{2,1,0:T(8,128)} %get-tuple-element.34), calls=%async_computation | async-start | bytes 65536 | tf_op jit(solution)/shard_map/all_to_all | solution.py:387
  22.6 1.2 %copy-start = (bf16[1,32,128,128]{3,2,1,0:T(8,128)(2,1)S(1)}, bf16[1,32,128,128]{3,2,1,0:T(8,128)(2,1)}, u32[]{:S(2)}) copy-start(bf16[1,32,128,128]{3,2,1,0:T(8,128)(2,1)} %param.9) | copy-start | bytes 3145732
  23.9 3.2 %copy-start.2 = (bf16[1,32,128,128]{3,2,1,0:T(8,128)(2,1)S(1)}, bf16[1,32,128,128]{3,2,1,0:T(8,128)(2,1)}, u32[]{:S(2)}) copy-start(bf16[1,32,128,128]{3,2,1,0:T(8,128)(2,1)} %param.10) | copy-start | bytes 3145732
  27.1 11.5 %copy-start.5 = (f32[128]{0:T(128)S(1)}, f32[128]{0:T(128)}, u32[]{:S(2)}) copy-start(f32[128]{0:T(128)} %param.15) | copy-start | bytes 1540
  27.1 11.5 %copy-start.7 = (f32[128]{0:T(128)S(1)}, f32[128]{0:T(128)}, u32[]{:S(2)}) copy-start(f32[128]{0:T(128)} %param.16) | copy-start | bytes 1540
  40.3 14.0 %collective-permute-start.2 = (f32[2,128,128]{2,1,0:T(8,128)S(1)}, f32[2,128,128]{2,1,0:T(8,128)S(1)}, u32[]{:S(2)}, u32[]{:S(2)}) collective-permute-start(f32[2,128,128]{2,1,0:T(8,128)S(1)} %get-tuple-element.52), channel_id=1, source_target_pairs={{0,1},{1,2},{2,3},{3,4},{4,5},{5,6},{6,7},{7,0},{8,9},{9,10},{10,1... | collective-permute-start | bytes 393224 | tf_op jit(solution)/shard_map/ppermute | solution.py:391
  40.6 13.6 %collective-permute-start.3 = (f32[2,128,128]{2,1,0:T(8,128)S(1)}, f32[2,128,128]{2,1,0:T(8,128)S(1)}, u32[]{:S(2)}, u32[]{:S(2)}) collective-permute-start(f32[2,128,128]{2,1,0:T(8,128)S(1)} %get-tuple-element.53), channel_id=1, source_target_pairs={{0,7},{1,0},{2,1},{3,2},{4,3},{5,4},{6,5},{7,6},{8,15},{9,8},{10,9... | collective-permute-start | bytes 393224 | tf_op jit(solution)/shard_map/ppermute | solution.py:391
  43.0 11.2 %copy-start.1 = (bf16[1,32,128,128]{3,2,1,0:T(8,128)(2,1)S(1)}, bf16[1,32,128,128]{3,2,1,0:T(8,128)(2,1)}, u32[]{:S(2)}) copy-start(bf16[1,32,128,128]{3,2,1,0:T(8,128)(2,1)} %param.9) | copy-start | bytes 3145732

commit v3 on v2

--- a/solution.py
+++ b/solution.py
@@ -20,6 +20,7 @@
 CELLS = float(HEIGHT * COLS * PER_GROUP)
 WIDE = 3 * CH
 PAIR = 2 * WIDE
+STEPS = 4
 MIB = 1 << 20
 
 VMEM = pl.BlockSpec(memory_space=pltpu.VMEM)
@@ -84,26 +85,21 @@
         out_ref[j] = tile
 
 
-def channel_stats(load, length, out_ref):
-    def first(i, acc):
-        for k in range(4):
-            r = i * 4 + k
-            acc = acc + jnp.where(r < length, sums8(load(r)), 0.0)
-        return acc
-
-    total = jnp.sum(lax.fori_loop(0, SLOTS // 4, first, jnp.zeros((8, CH), F32)), axis=0, keepdims=True)
+def kept_sums(value, r, length):
+    return jnp.where(r < length, sums8(value), 0.0)
+
+
+def channel_stats(load, length, out_ref, total=None):
+    if total is None:
+        total = sum(kept_sums(load(r), r, length) for r in range(SLOTS))
+    total = jnp.sum(total, axis=0, keepdims=True)
     used = length.astype(F32)
     mean = total / (used * float(COLS))
-
-    def second(i, acc):
-        for k in range(4):
-            r = i * 4 + k
-            gap = load(r) - mean
-            acc = acc + jnp.where(r < length, sums8(gap * gap), 0.0)
-        return acc
-
-    spread = jnp.sum(lax.fori_loop(0, SLOTS // 4, second, jnp.zeros((8, CH), F32)), axis=0, keepdims=True)
-    send(out_ref, [total, spread, jnp.broadcast_to(used, (1, CH))])
+    spread = jnp.zeros((8, CH), F32)
+    for r in range(SLOTS):
+        gap = load(r) - mean
+        spread = spread + kept_sums(gap * gap, r, length)
+    send(out_ref, [total, jnp.sum(spread, axis=0, keepdims=True), jnp.broadcast_to(used, (1, CH))])
 
 
 def sigmoid(z):
@@ -111,9 +107,10 @@
 
 
 def taps(row):
-    col = lax.broadcasted_iota(jnp.int32, (COLS, CH), 0)
-    before = jnp.where(col == 0, 0.0, pltpu.roll(row, 1, 0))
-    after = jnp.where(col == COLS - 1, 0.0, pltpu.roll(row, COLS - 1, 0))
+    col = lax.broadcasted_iota(jnp.int32, (8, CH), 0)
+    before, after = pltpu.roll(row, 1, 0), pltpu.roll(row, COLS - 1, 0)
+    before = jnp.concatenate([jnp.where(col == 0, 0.0, before[0:8]), before[8:]], axis=0)
+    after = jnp.concatenate([after[:-8], jnp.where(col == 7, 0.0, after[-8:])], axis=0)
     return jnp.concatenate([before.astype(BF16), row.astype(BF16), after.astype(BF16)], axis=1)
 
 
@@ -127,8 +124,9 @@
         beside(begin // chunk)
         upper = buf[begin : begin + chunk].reshape(chunk * COLS, PAIR)
         lower = buf[begin + 1 : begin + 1 + chunk].reshape(chunk * COLS, PAIR)
-        out = jnp.dot(upper, w_ref[0], preferred_element_type=F32)
-        out = out + jnp.dot(lower, w_ref[1], preferred_element_type=F32)
+        out = jnp.dot(
+            jnp.concatenate([upper, lower], axis=1), w_ref[...].reshape(2 * PAIR, 2 * CH), preferred_element_type=F32
+        )
         out = out.reshape(chunk, COLS, 2 * CH)
         for k in range(chunk):
             finish(2 * (begin + k), out[k, :, 0:CH])
@@ -167,17 +165,23 @@
 def stats_kernel(len_ref, x_ref, g_ref, top_ref, bottom_ref, out_ref, rows_ref, sem, edge_sem):
     length = len_ref[0, 0]
     last = length - 1
-    whole = pltpu.make_async_copy(x_ref, rows_ref, sem)
-    whole.start()
+    step = SLOTS // STEPS
     started = []
+    for k in range(STEPS):
+        part = pl.ds(k * step, step)
+        started.append(pltpu.make_async_copy(x_ref.at[part], rows_ref.at[part], sem.at[k]))
     for k, ref in enumerate((x_ref, g_ref)):
         started.append(pltpu.make_async_copy(ref.at[0], top_ref.at[k], edge_sem.at[2 * k]))
         started.append(pltpu.make_async_copy(ref.at[last], bottom_ref.at[k], edge_sem.at[2 * k + 1]))
     for copy in started:
         copy.start()
-    whole.wait()
-    channel_stats(lambda r: rows_ref[r].astype(F32), length, out_ref)
-    for copy in started:
+    total = jnp.zeros((8, CH), F32)
+    for k in range(STEPS):
+        started[k].wait()
+        for r in range(k * step, (k + 1) * step):
+            total = total + kept_sums(rows_ref[r].astype(F32), r, length)
+    channel_stats(lambda r: rows_ref[r].astype(F32), length, out_ref, total)
+    for copy in started[STEPS:]:
         copy.wait()
 
 
@@ -198,9 +202,9 @@
 
 
 def hidden_kernel(
-    len_ref, strip_ref, x_ref, up_ref, down_ref, st_ref, w_ref, gain_ref, shift_ref, hid_ref, act_ref, out_ref
+    len_ref, x_ref, up_ref, down_ref, st_ref, w_ref, gain_ref, shift_ref, hid_ref, act_ref, out_ref
 ):
-    length, strip = len_ref[0, 0], strip_ref[0]
+    length, strip = len_ref[0, 0], lax.axis_index("strip")
     mean, inv = group_stats(st_ref)
     scale, shift = inv * gain_ref[...], shift_ref[...]
 
@@ -209,15 +213,18 @@
         pre = (row.astype(F32) - mean) * scale + shift
         return jnp.where(in_image(length, strip, t), pre * sigmoid(pre), 0.0)
 
+    total = [jnp.zeros((8, CH), F32)]
+
     def finish(r, row):
         hid_ref[r] = row
+        total[0] = total[0] + kept_sums(row, r, length)
 
     convolve(act_ref, w_ref, row_at, finish)
-    channel_stats(lambda r: hid_ref[r], length, out_ref)
-
-
-def back_kernel(len_ref, strip_ref, g_ref, up_ref, down_ref, w_ref, act_ref, g_taps_ref, back_ref, act_t_ref):
-    length, strip = len_ref[0, 0], strip_ref[0]
+    channel_stats(lambda r: hid_ref[r], length, out_ref, total[0])
+
+
+def back_kernel(len_ref, g_ref, up_ref, down_ref, w_ref, act_ref, g_taps_ref, back_ref, act_t_ref):
+    length, strip = len_ref[0, 0], lax.axis_index("strip")
 
     def row_at(t):
         row = around(lambda r: g_ref[r], up_ref[1], down_ref[1], length, t)
@@ -241,23 +248,17 @@
     mean, inv = group_stats(st_ref)
     gain, shift = gain_ref[...], shift_ref[...]
 
-    def step(i, carry):
-        cross, plain = carry
-        for k in range(2):
-            r = 2 * i + k
-            normed = (hid_ref[r] - mean) * inv
-            pre = normed * gain + shift
-            s = sigmoid(pre)
-            act = pre * s
-            act_ref[r] = act.astype(BF16)
-            grad = jnp.where(r < length, back_ref[r] * (s + act * (1.0 - s)), 0.0)
-            dpre_ref[r] = grad
-            plain = plain + sums8(grad)
-            cross = cross + sums8(grad * normed)
-        return cross, plain
-
-    zero = jnp.zeros((8, CH), F32)
-    cross, plain = lax.fori_loop(0, SLOTS // 2, step, (zero, zero))
+    cross = plain = jnp.zeros((8, CH), F32)
+    for r in range(SLOTS):
+        normed = (hid_ref[r] - mean) * inv
+        pre = normed * gain + shift
+        s = sigmoid(pre)
+        act = pre * s
+        act_ref[r] = act.astype(BF16)
+        grad = jnp.where(r < length, back_ref[r] * (s + act * (1.0 - s)), 0.0)
+        dpre_ref[r] = grad
+        plain = plain + sums8(grad)
+        cross = cross + sums8(grad * normed)
     send(out_ref, [jnp.sum(cross, axis=0, keepdims=True), jnp.sum(plain, axis=0, keepdims=True)])
     for ref, row in ((top_ref, 0), (bottom_ref, length - 1)):
         ref[0] = dpre_ref[row]
@@ -278,18 +279,20 @@
 
 
 def dpre1_kernel(
-    len_ref, strip_ref, st1_ref, st2_ref, sums_ref, own_sums_ref, hid_ref, dpre2_ref, up_ref, down_ref, act_t_ref,
+    len_ref, st1_ref, st2_ref, sums_ref, own_sums_ref, hid_ref, dpre2_ref, up_ref, down_ref, act_t_ref,
     x_ref, grad2_ref, w_ref, gain1_ref, shift1_ref, gain2_ref,
     share_ref, dpre_ref, out_ref, d_taps_ref, grad1_ref,
 ):
-    length, strip = len_ref[0, 0], strip_ref[0]
+    length, strip = len_ref[0, 0], lax.axis_index("strip")
     half = SLOTS // 2
     mean2, inv2 = group_stats(st2_ref)
     gain2 = gain2_ref[...]
     cross2, plain2 = moments(sums_ref, gain2)
 
+    by_dpre, by_hidden, level = inv2 * gain2, inv2 * inv2 * cross2, inv2 * plain2
+
     def dhidden(dpre, hidden):
-        return inv2 * (dpre * gain2 - plain2 - (hidden - mean2) * inv2 * cross2)
+        return dpre * by_dpre - (hidden - mean2) * by_hidden - level
 
     mean1, inv1 = group_stats(st1_ref)
     gain1, shift1 = gain1_ref[...], shift1_ref[...]
@@ -358,29 +361,34 @@
 
 
 def finish_kernel(
-    len_ref, in_ref, st_ref, x_ref, g_ref, dpre_ref, gain_ref, image_ref, first_ref, second_ref, norm_ref
+    len_ref, in_ref, st_ref, x_ref, g_ref, dpre_ref, gain_ref, image_ref, first_ref, second_ref, norm_ref,
+    rows_ref, first_own, second_own, norm_own, sem,
 ):
     total = in_ref[0].astype(F32)
     for j in range(1, PEERS):
         total = total + in_ref[j].astype(F32)
     rows = first_ref.shape[0]
-    first_ref[...], second_ref[...], norm_ref[...] = unpacked(total[0 : 2 * rows + 8])
+    first_own[...], second_own[...], norm_own[...] = unpacked(total[0 : 2 * rows + 8])
+    copies = []
+    for k, (own, ref) in enumerate(((first_own, first_ref), (second_own, second_ref), (norm_own, norm_ref))):
+        copies.append(pltpu.make_async_copy(own, ref, sem.at[STEPS + k]))
+        copies[k].start()
     sums = total[2 * rows + 8 : 2 * rows + 12] + total[2 * rows + 12 : 2 * rows + 16]
     length = len_ref[0, 0]
     mean, inv = group_stats(st_ref)
     gain = gain_ref[...]
     cross, plain = folded(sums[0:1] * gain) / CELLS, folded(sums[1:2] * gain) / CELLS
-
-    def step(i, carry):
-        for k in range(2):
-            r = 2 * i + k
-            normed = (x_ref[r].astype(F32) - mean) * inv
-            grad = inv * (dpre_ref[r] * gain - plain - normed * cross)
-            grad = jnp.where(r < length, g_ref[r].astype(F32) + grad, 0.0)
-            image_ref[r] = grad.astype(BF16)
-        return carry
-
-    lax.fori_loop(0, SLOTS // 2, step, 0)
+    by_dpre, by_x, level = inv * gain, inv * inv * cross, inv * plain
+    step = SLOTS // STEPS
+    for k in range(STEPS):
+        for r in range(k * step, (k + 1) * step):
+            grad = dpre_ref[r] * by_dpre - (x_ref[r].astype(F32) - mean) * by_x - level
+            rows_ref[r] = jnp.where(r < length, g_ref[r].astype(F32) + grad, 0.0).astype(BF16)
+        part = pl.ds(k * step, step)
+        copies.append(pltpu.make_async_copy(rows_ref.at[part], image_ref.at[part], sem.at[k]))
+        copies[-1].start()
+    for copy in copies:
+        copy.wait()
 
 
 def exchanged(value, axis):
@@ -397,8 +405,6 @@
     x, g = image_in[0], cotangent[0]
     gain1, shift1 = norm1_gain[None], norm1_shift[None]
     gain2, shift2 = norm2_gain[None], norm2_shift[None]
-    strip = lax.axis_index("strip")
-    strip_id = strip.reshape(1).astype(jnp.int32)
     images = lax.axis_size(IMG)
     half = SLOTS // 2
     field = SLOTS * COLS * CH
@@ -412,7 +418,7 @@
         [shape((2, *edge), BF16), shape((2, *edge), BF16), stat],
         flops=field * 6,
         moved=field * 2,
-        scratch=[pltpu.VMEM((SLOTS, *edge), BF16), pltpu.SemaphoreType.DMA, pltpu.SemaphoreType.DMA((4,))],
+        scratch=[pltpu.VMEM((SLOTS, *edge), BF16), pltpu.SemaphoreType.DMA((STEPS,)), pltpu.SemaphoreType.DMA((4,))],
         limit=63 * MIB + MIB // 4,
     )(strip_rows, x, g)
     up, down = shifted(bottom, 1), shifted(top, -1)
@@ -423,15 +429,15 @@
 
     hidden, act1, stats2 = call(
         hidden_kernel,
-        [SMEM, SMEM] + [VMEM] * 7,
+        [SMEM] + [VMEM] * 7,
         [shape((SLOTS, *edge), F32), shape((half + 1, COLS, PAIR), BF16), stat],
         flops=conv_flops,
         moved=field * 6,
-    )(strip_rows, strip_id, x, up, down, stats1, weights1, gain1, shift1)
+    )(strip_rows, x, up, down, stats1, weights1, gain1, shift1)
 
     g_taps, back2, act1_t = call(
         back_kernel,
-        [SMEM, SMEM] + [VMEM] * 5,
+        [SMEM] + [VMEM] * 5,
         [
             shape((half + 1, COLS, PAIR), BF16),
             shape((SLOTS, *edge), F32),
@@ -439,7 +445,7 @@
         ],
         flops=conv_flops,
         moved=field * 6,
-    )(strip_rows, strip_id, g, up, down, turned2, act1)
+    )(strip_rows, g, up, down, turned2, act1)
     stats2, g_taps, back2, act1_t = lax.optimization_barrier((stats2, g_taps, back2, act1_t))
     stats2 = exchanged(stats2, "strip")
 
@@ -468,13 +474,13 @@
     rows = 9 * CH // images
     share, dpre1, own_sums1 = call(
         dpre1_kernel,
-        [SMEM, SMEM] + [VMEM] * 15,
+        [SMEM] + [VMEM] * 15,
         [shape((images, 2 * rows + 8, CH), BF16), shape((SLOTS, *edge), F32), shape((8, CH), F32)],
         flops=2 * conv_flops,
         moved=field * 8,
         scratch=[pltpu.VMEM((half + 1, COLS, PAIR), BF16), pltpu.VMEM((WIDE, WIDE), F32)],
     )(
-        strip_rows, strip_id, stats1, stats2, sums2, own_sums2, hidden, dpre2, up, down, act1_t, x, grad2, turned1,
+        strip_rows, stats1, stats2, sums2, own_sums2, hidden, dpre2, up, down, act1_t, x, grad2, turned1,
         gain1, shift1, gain2,
     )
     share, dpre1, own_sums1 = lax.optimization_barrier((share, dpre1, own_sums1))
@@ -489,6 +495,11 @@
         [shape((SLOTS, *edge), BF16), shape((rows, CH), F32), shape((rows, CH), F32), shape((4, CH), F32)],
         flops=field * 12,
         moved=field * 10,
+        scratch=[
+            pltpu.VMEM((SLOTS, *edge), BF16), pltpu.VMEM((rows, CH), F32), pltpu.VMEM((rows, CH), F32),
+            pltpu.VMEM((4, CH), F32), pltpu.SemaphoreType.DMA((STEPS + 3,)),
+        ],
+        outs_in=[HBM] * 4,
     )(strip_rows, relayed, stats1, x, g, dpre1, gain1)
     return image_grad[None], grad1, grad2, norm_grads
 

time: 99.2 us -> 98.3 us (level)
  Pallas kernels: 19.6 us -> 18.4 us
where the time goes in v3:
time: 98.3 us; the launch traced here: 97.9 us
  blocking collectives  55.6 us (57%)
  Pallas kernels  18.4 us (19%)
  starting transfers between devices  14.5 us (15%)
  waiting for transfers between devices  6.54 us (7%)
  between operations  1.64 us (2%)
  local copies, waits for them, and re-layouts  1.26 us (1%)
    all_to_all x4, blocking collectives, exchanged(): return lax.all_to_all(value, axis, split_axis=0, concat_axis=0, tiled=True)  55.6 us
    ppermute x4, starting transfers between devices, shifted(): lax.ppermute(value, 'strip', [(i, (i + by) % PEERS) for i in range(PEERS)])  9.31 us
    all_to_all x1, waiting for transfers between devices, exchanged(): return lax.all_to_all(value, axis, split_axis=0, concat_axis=0, tiled=True)  6.53 us
    all_to_all x1, starting transfers between devices, exchanged(): return lax.all_to_all(value, axis, split_axis=0, concat_axis=0, tiled=True)  5.2 us
    pallas_call x1, Pallas kernels, body(): call(dpre1_kernel, [SMEM] + [VMEM] * 15, [shape((images, 2 * rows + 8, CH...  5.2 us
    pallas_call x1, Pallas kernels, body(): call(hidden_kernel, [SMEM] + [VMEM] * 7, [shape((SLOTS, *edge), F32), sha...  2.93 us
    pallas_call x1, Pallas kernels, body(): call(stats_kernel, [SMEM, HBM, HBM], [shape((2, *edge), BF16), shape((2,...  2.29 us
    pallas_call x1, Pallas kernels, body(): call(back_kernel, [SMEM] + [VMEM] * 5, [shape((half + 1, COLS, PAIR), BF1...  2.23 us
  transfers between devices with their start and end apart: 5, of which 1 were waited for; matrix products, arithmetic and copies ran while one was open for 0% of the time, Pallas kernels for 2%

profile of v3, /device:TPU:1, one launch (start us, length us, event | category | flops | bytes accessed | tf_op | source)
XLA Modules:
  0.0 97.9 jit_solution(11450763462038832690)
XLA Ops:
  0.6 0.0 copy-start.4
  0.6 0.0 copy-start.3
  0.7 0.0 copy-start.8
  0.7 0.0 copy-start.6
  1.4 2.3 %shard_map.120 = (bf16[2,128,128]{2,1,0:T(8,128)(2,1)}, bf16[2,128,128]{2,1,0:T(8,128)(2,1)}, f32[8,8,128]{2,1,0:T(8,128)}) custom-call(s32[1,1]{1,0:T(1,128)S(6)} %copy.13.len_ref, bf16[32,128,128]{2,1,0:T(8,128)(2,1)} %bitcast.7, bf16[32,128,128]{2,1,0:T(8,128)(2,1)} %bitcast.11), custom_call_target="tpu_custom_call" | custom-call | flops 3145728 | bytes 1048576 | tf_op jit(solution)/shard_map/pallas_call | solution.py:415
  3.7 2.5 %collective-permute-start = (bf16[2,128,128]{2,1,0:T(8,128)(2,1)}, bf16[2,128,128]{2,1,0:T(8,128)(2,1)S(1)}, u32[]{:S(2)}, u32[]{:S(2)}) collective-permute-start(bf16[2,128,128]{2,1,0:T(8,128)(2,1)} %get-tuple-element.35), channel_id=1, source_target_pairs={{0,1},{1,2},{2,3},{3,4},{4,5},{5,6},{6,7},{7,0},{8,9},{9,10},{10,1... | collective-permute-start | bytes 196616 | tf_op jit(solution)/shard_map/ppermute | solution.py:399
  6.2 4.0 %collective-permute-start.1 = (bf16[2,128,128]{2,1,0:T(8,128)(2,1)}, bf16[2,128,128]{2,1,0:T(8,128)(2,1)S(1)}, u32[]{:S(2)}, u32[]{:S(2)}) collective-permute-start(bf16[2,128,128]{2,1,0:T(8,128)(2,1)} %get-tuple-element.36), channel_id=1, source_target_pairs={{0,7},{1,0},{2,1},{3,2},{4,3},{5,4},{6,5},{7,6},{8,15},{9,8},{10,9... | collective-permute-start | bytes 196616 | tf_op jit(solution)/shard_map/ppermute | solution.py:399
  10.2 5.2 %all-to-all-start = ((f32[8,8,128]{2,1,0:T(8,128)}), f32[8,8,128]{2,1,0:T(8,128)S(1)}, u32[]{:S(2)}, u32[]{:S(2)}) async-start(f32[8,8,128]{2,1,0:T(8,128)} %get-tuple-element.34), calls=%async_computation | async-start | bytes 65536 | tf_op jit(solution)/shard_map/all_to_all | solution.py:395
  15.4 0.0 copy-done.4
  15.4 0.0 copy-done.3
  15.4 0.4 shard_map.121
  15.8 6.5 %all-to-all-done.st_ref.st1_ref = f32[8,8,128]{2,1,0:T(8,128)S(1)} async-done(((f32[8,8,128]{2,1,0:T(8,128)}), f32[8,8,128]{2,1,0:T(8,128)S(1)}, u32[]{:S(2)}, u32[]{:S(2)}) %all-to-all-start) | async-done | bytes 32800 | tf_op jit(solution)/shard_map/all_to_all | solution.py:395
  22.3 0.0 collective-permute-done.up_ref
  22.3 0.0 collective-permute-done.1.down_ref
  22.3 0.0 copy-done.8
  22.4 0.0 copy-done.6
  22.4 0.0 copy-start
  22.4 1.2 %copy-done = bf16[1,32,128,128]{3,2,1,0:T(8,128)(2,1)S(1)} copy-done((bf16[1,32,128,128]{3,2,1,0:T(8,128)(2,1)S(1)}, bf16[1,32,128,128]{3,2,1,0:T(8,128)(2,1)}, u32[]{:S(2)}) %copy-start) | copy-done | bytes 1048600
  23.6 0.0 copy-start.2
  23.6 2.9 %shard_map.122 = (f32[32,128,128]{2,1,0:T(8,128)S(1)}, bf16[17,128,768]{2,1,0:T(8,128)(2,1)S(1)}, f32[8,8,128]{2,1,0:T(8,128)S(1)}) custom-call(s32[1,1]{1,0:T(1,128)S(6)} %copy.13.len_ref, bf16[32,128,128]{2,1,0:T(8,128)(2,1)S(1)} %bitcast.8, bf16[2,128,128]{2,1,0:T(8,128)(2,1)S(1)} %collective-permute-done.up_ref, ...), custom_call_target="tpu_custom_call" | custom-call | flops 1207959552 | bytes 3145728 | tf_op jit(solution)/shard_map/pallas_call | solution.py:430
  26.5 0.0 copy-done.2
  26.5 0.0 copy-start.5
  26.5 0.0 copy-start.7
  26.6 2.2 %shard_map.123 = (bf16[17,128,768]{2,1,0:T(8,128)(2,1)S(1)}, f32[32,128,128]{2,1,0:T(8,128)S(1)}, bf16[2,384,2304]{2,1,0:T(8,128)(2,1)S(1)}) custom-call(s32[1,1]{1,0:T(1,128)S(6)} %copy.13.len_ref, bf16[32,128,128]{2,1,0:T(8,128)(2,1)S(1)} %bitcast.12, bf16[2,128,128]{2,1,0:T(8,128)(2,1)S(1)} %collective-permute-done.up_ref, ...), custom_call_target="tpu_custom_call" | custom-call | flops 1207959552 | bytes 3145728 | tf_op jit(solution)/shard_map/pallas_call | solution.py:438
  28.8 9.2 %all_to_all.25.st_ref.st2_ref = f32[8,8,128]{2,1,0:T(8,128)S(1)} all-to-all(f32[8,8,128]{2,1,0:T(8,128)S(1)} %get-tuple-element.44), channel_id=1, replica_groups=mesh['img_0'=4,'img_1'=4,'img_2'=2,'strip'=8] {'strip'}, dimensions={0} | all-to-all | bytes 65536 | tf_op jit(solution)/shard_map/all_to_all | solution.py:395
  38.0 0.0 copy-done.5
  38.0 0.0 copy-done.7
  38.0 1.6 %shard_map.124 = (bf16[32,128,128]{2,1,0:T(8,128)(2,1)S(1)}, f32[32,128,128]{2,1,0:T(8,128)S(1)}, f32[2,128,128]{2,1,0:T(8,128)S(1)}, f32[2,128,128]{2,1,0:T(8,128)S(1)}, f32[8,8,128]{2,1,0:T(8,128)S(1)}) custom-call(s32[1,1]{1,0:T(1,128)S(6)} %copy.13.len_ref, f32[8,8,128]{2,1,0:T(8,128)S(1)} %all_to_all.25.st_ref.st2_ref, ...), custom_call_target="tpu_custom_call" | custom-call | flops 20971520 | bytes 4194304 | tf_op jit(solution)/shard_map/pallas_call | solution.py:452
  39.7 0.4 collective-permute-start.2
  40.1 2.4 %collective-permute-start.3 = (f32[2,128,128]{2,1,0:T(8,128)S(1)}, f32[2,128,128]{2,1,0:T(8,128)S(1)}, u32[]{:S(2)}, u32[]{:S(2)}) collective-permute-start(f32[2,128,128]{2,1,0:T(8,128)S(1)} %get-tuple-element.53), channel_id=1, source_target_pairs={{0,7},{1,0},{2,1},{3,2},{4,3},{5,4},{6,5},{7,6},{8,15},{9,8},{10,9... | collective-permute-start | bytes 393224 | tf_op jit(solution)/shard_map/ppermute | solution.py:399
  42.4 0.0 copy-start.1
  42.4 2.0 %shard_map.125.grad2_ref = f32[384,384]{1,0:T(8,128)S(1)} custom-call(s32[1,1]{1,0:T(1,128)S(6)} %copy.13.len_ref, bf16[32,128,128]{2,1,0:T(8,128)(2,1)S(1)} %get-tuple-element.48.act_ref, bf16[17,128,768]{2,1,0:T(8,128)(2,1)S(1)} %get-tuple-element.49.g_taps_ref), custom_call_target="tpu_custom_call" | custom-call | flops 1207959552 | bytes 3145728 | tf_op jit(solution)/shard_map/pallas_call | solution.py:463
  44.4 9.4 %all_to_all.26.sums_ref = f32[8,8,128]{2,1,0:T(8,128)S(1)} all-to-all(f32[8,8,128]{2,1,0:T(8,128)S(1)} %get-tuple-element.50.own_sums_ref), channel_id=1, replica_groups=mesh['img_0'=4,'img_1'=4,'img_2'=2,'strip'=8] {'strip'}, dimensions={0} | all-to-all | bytes 65536 | tf_op jit(solution)/shard_map/all_to_all | solution.py:395
  53.9 0.0 collective-permute-done.2.up_ref
  53.9 0.0 collective-permute-done.3.down_ref
  53.9 0.0 copy-done.1
  53.9 5.2 %shard_map.126 = (bf16[32,80,128]{2,1,0:T(8,128)(2,1)S(1)}, f32[32,128,128]{2,1,0:T(8,128)S(1)}, f32[8,128]{1,0:T(8,128)S(1)}) custom-call(s32[1,1]{1,0:T(1,128)S(6)} %copy.13.len_ref, f32[8,8,128]{2,1,0:T(8,128)S(1)} %all-to-all-done.st_ref.st1_ref, f32[8,8,128]{2,1,0:T(8,128)S(1)} %all_to_all.25.st_ref.st2_ref, f32[8,8,128]{2,1,0:T(8,128)S(1)} %all_to_all.26.sums_ref, ...), custom_call_target="tpu_custom_call" | custom-call | flops 2415919104 | bytes 4194304 | tf_op jit(solution)/shard_map/pallas_call | solution.py:475
  59.1 25.2 %all_to_all.27.in_ref = bf16[32,80,128]{2,1,0:T(8,128)(2,1)S(1)} all-to-all(bf16[32,80,128]{2,1,0:T(8,128)(2,1)S(1)} %get-tuple-element.57), channel_id=1, replica_groups=mesh['img_0'=4,'img_1'=4,'img_2'=2,'strip'=8] {'img_0','img_1','img_2'}, dimensions={0} | all-to-all | bytes 1310720 | tf_op jit(solution)/shard_map/all_to_all | solution.py:395
  84.3 0.1 shard_map.127
  84.4 11.7 %all_to_all.28.in_ref = bf16[8,88,128]{2,1,0:T(8,128)(2,1)S(1)} all-to-all(bf16[8,88,128]{2,1,0:T(8,128)(2,1)S(1)} %shard_map.127), channel_id=1, replica_groups=mesh['img_0'=4,'img_1'=4,'img_2'=2,'strip'=8] {'strip'}, dimensions={0} | all-to-all | bytes 360448 | tf_op jit(solution)/shard_map/all_to_all | solution.py:395
  96.1 1.7 %shard_map.128 = (bf16[32,128,128]{2,1,0:T(8,128)(2,1)}, f32[36,128]{1,0:T(8,128)}, f32[36,128]{1,0:T(8,128)}, f32[4,128]{1,0:T(4,128)}) custom-call(s32[1,1]{1,0:T(1,128)S(6)} %copy.13.len_ref, bf16[8,88,128]{2,1,0:T(8,128)(2,1)S(1)} %all_to_all.28.in_ref, f32[8,8,128]{2,1,0:T(8,128)S(1)} %all-to-all-done.st_ref.st1_ref, ...), custom_call_target="tpu_custom_call" | custom-call | flops 6291456 | bytes 5242880 | tf_op jit(solution)/shard_map/pallas_call | solution.py:492
Async XLA Ops:
  0.6 14.8 %copy-start.4 = (bf16[3,3,128,128]{3,2,1,0:T(8,128)(2,1)S(1)}, bf16[3,3,128,128]{3,2,1,0:T(8,128)(2,1)}, u32[]{:S(2)}) copy-start(bf16[3,3,128,128]{3,2,1,0:T(8,128)(2,1)} %second_ref.1) | copy-start | bytes 884740
  0.6 14.8 %copy-start.3 = (bf16[3,3,128,128]{3,2,1,0:T(8,128)(2,1)S(1)}, bf16[3,3,128,128]{3,2,1,0:T(8,128)(2,1)}, u32[]{:S(2)}) copy-start(bf16[3,3,128,128]{3,2,1,0:T(8,128)(2,1)} %first_ref.1) | copy-start | bytes 884740
  0.7 21.7 %copy-start.8 = (f32[128]{0:T(128)S(1)}, f32[128]{0:T(128)}, u32[]{:S(2)}) copy-start(f32[128]{0:T(128)} %param.14) | copy-start | bytes 1540
  0.7 21.7 %copy-start.6 = (f32[128]{0:T(128)S(1)}, f32[128]{0:T(128)}, u32[]{:S(2)}) copy-start(f32[128]{0:T(128)} %param.13) | copy-start | bytes 1540
  3.7 18.7 %collective-permute-start = (bf16[2,128,128]{2,1,0:T(8,128)(2,1)}, bf16[2,128,128]{2,1,0:T(8,128)(2,1)S(1)}, u32[]{:S(2)}, u32[]{:S(2)}) collective-permute-start(bf16[2,128,128]{2,1,0:T(8,128)(2,1)} %get-tuple-element.35), channel_id=1, source_target_pairs={{0,1},{1,2},{2,3},{3,4},{4,5},{5,6},{6,7},{7,0},{8,9},{9,10},{10,1... | collective-permute-start | bytes 196616 | tf_op jit(solution)/shard_map/ppermute | solution.py:399
  6.2 16.1 %collective-permute-start.1 = (bf16[2,128,128]{2,1,0:T(8,128)(2,1)}, bf16[2,128,128]{2,1,0:T(8,128)(2,1)S(1)}, u32[]{:S(2)}, u32[]{:S(2)}) collective-permute-start(bf16[2,128,128]{2,1,0:T(8,128)(2,1)} %get-tuple-element.36), channel_id=1, source_target_pairs={{0,7},{1,0},{2,1},{3,2},{4,3},{5,4},{6,5},{7,6},{8,15},{9,8},{10,9... | collective-permute-start | bytes 196616 | tf_op jit(solution)/shard_map/ppermute | solution.py:399
  10.2 12.1 %all-to-all-start = ((f32[8,8,128]{2,1,0:T(8,128)}), f32[8,8,128]{2,1,0:T(8,128)S(1)}, u32[]{:S(2)}, u32[]{:S(2)}) async-start(f32[8,8,128]{2,1,0:T(8,128)} %get-tuple-element.34), calls=%async_computation | async-start | bytes 65536 | tf_op jit(solution)/shard_map/all_to_all | solution.py:395
  22.4 1.2 %copy-start = (bf16[1,32,128,128]{3,2,1,0:T(8,128)(2,1)S(1)}, bf16[1,32,128,128]{3,2,1,0:T(8,128)(2,1)}, u32[]{:S(2)}) copy-start(bf16[1,32,128,128]{3,2,1,0:T(8,128)(2,1)} %param.9) | copy-start | bytes 3145732
  23.6 2.9 %copy-start.2 = (bf16[1,32,128,128]{3,2,1,0:T(8,128)(2,1)S(1)}, bf16[1,32,128,128]{3,2,1,0:T(8,128)(2,1)}, u32[]{:S(2)}) copy-start(bf16[1,32,128,128]{3,2,1,0:T(8,128)(2,1)} %param.10) | copy-start | bytes 3145732
  26.5 11.5 %copy-start.5 = (f32[128]{0:T(128)S(1)}, f32[128]{0:T(128)}, u32[]{:S(2)}) copy-start(f32[128]{0:T(128)} %param.15) | copy-start | bytes 1540
  26.5 11.5 %copy-start.7 = (f32[128]{0:T(128)S(1)}, f32[128]{0:T(128)}, u32[]{:S(2)}) copy-start(f32[128]{0:T(128)} %param.16) | copy-start | bytes 1540
  39.7 14.2 %collective-permute-start.2 = (f32[2,128,128]{2,1,0:T(8,128)S(1)}, f32[2,128,128]{2,1,0:T(8,128)S(1)}, u32[]{:S(2)}, u32[]{:S(2)}) collective-permute-start(f32[2,128,128]{2,1,0:T(8,128)S(1)} %get-tuple-element.52), channel_id=1, source_target_pairs={{0,1},{1,2},{2,3},{3,4},{4,5},{5,6},{6,7},{7,0},{8,9},{9,10},{10,1... | collective-permute-start | bytes 393224 | tf_op jit(solution)/shard_map/ppermute | solution.py:399
  40.1 13.8 %collective-permute-start.3 = (f32[2,128,128]{2,1,0:T(8,128)S(1)}, f32[2,128,128]{2,1,0:T(8,128)S(1)}, u32[]{:S(2)}, u32[]{:S(2)}) collective-permute-start(f32[2,128,128]{2,1,0:T(8,128)S(1)} %get-tuple-element.53), channel_id=1, source_target_pairs={{0,7},{1,0},{2,1},{3,2},{4,3},{5,4},{6,5},{7,6},{8,15},{9,8},{10,9... | collective-permute-start | bytes 393224 | tf_op jit(solution)/shard_map/ppermute | solution.py:399
  42.4 11.4 %copy-start.1 = (bf16[1,32,128,128]{3,2,1,0:T(8,128)(2,1)S(1)}, bf16[1,32,128,128]{3,2,1,0:T(8,128)(2,1)}, u32[]{:S(2)}) copy-start(bf16[1,32,128,128]{3,2,1,0:T(8,128)(2,1)} %param.9) | copy-start | bytes 3145732
